TPU v7x, 32 devices: a whole 2x2x4 slice. The times are simulated.
32 devices in a mesh: dp: 2 (over x), ws: 16 (over z, y, core).
Axes of the slice: x: 2, y: 2, z: 4, core: 2. Of those that a mesh axis runs over, the one named last changes fastest.
Arguments:
- hidden: bfloat16 [256, 768], P(('dp', 'ws')), parts along dimension 0
- self_k: bfloat16 [256, 12, 192, 64], P(('dp', 'ws')), parts along dimension 0
- self_v: bfloat16 [256, 12, 192, 64], P(('dp', 'ws')), parts along dimension 0
- cross_k: bfloat16 [256, 12, 384, 64], P(('dp', 'ws')), parts along dimension 0
- cross_v: bfloat16 [256, 12, 384, 64], P(('dp', 'ws')), parts along dimension 0
- positions: int32 [256], P(('dp', 'ws')), parts along dimension 0
- enc_mask: int32 [256, 384], P(('dp', 'ws')), parts along dimension 0
- rel_bias: float32 [12, 192], replicated
- expert_idx: int32 [256], P(('dp', 'ws')), parts along dimension 0
- ln_self: float32 [768], replicated
- ln_cross: float32 [768], replicated
- ln_ffn: float32 [768], replicated
- wq_self: bfloat16 [768, 768], P(None, 'ws')
- wk_self: bfloat16 [768, 768], P(None, 'ws')
- wv_self: bfloat16 [768, 768], P(None, 'ws')
- wo_self: bfloat16 [768, 768], P(None, 'ws')
- wq_cross: bfloat16 [768, 768], P(None, 'ws')
- wo_cross: bfloat16 [768, 768], P(None, 'ws')
- w_router: float32 [768, 16], P(None, 'ws')
- w_in: bfloat16 [16, 768, 3072], P(None, None, 'ws')
- w_out: bfloat16 [16, 3072, 768], P(None, 'ws')
Outputs:
- output 1: bfloat16 [256, 768], P(('dp', 'ws')), parts along dimension 0
- output 2: bfloat16 [256, 12, 192, 64], P(('dp', 'ws')), parts along dimension 0
- output 3: bfloat16 [256, 12, 192, 64], P(('dp', 'ws')), parts along dimension 0
There are 2 independent parts. A program takes and returns all parts, laid end to end along the dimension named above; an argument that names none is the same for every part.
All inputs are finite; a program needn't handle non-finite values.
Results may differ from a plain program's by a relative error of at most 0.0111322.
Values are sent between devices in bfloat16 or wider.
A program may use at most 1 GiB of HBM per device.

v0:
```python
import functools
import jax
import jax.numpy as jnp
from jax import lax
from jax.sharding import PartitionSpec as P

EPSILON = 1e-6
NEG_BIG = -1e30


def rms_norm(hidden, scale):
    hid_f32 = hidden.astype(jnp.float32)
    inv_rms = lax.rsqrt(jnp.mean(hid_f32 * hid_f32, axis=-1, keepdims=True) + EPSILON)
    return (hid_f32 * inv_rms * scale).astype(jnp.bfloat16)


def project(x_norm, weight):
    return jnp.dot(x_norm, weight, preferred_element_type=jnp.float32).astype(jnp.bfloat16)


def attend(queries, cache_keys, cache_vals, score_bias):
    scores = jnp.einsum('bhd,bhld->bhl', queries, cache_keys, preferred_element_type=jnp.float32) + score_bias
    attn_probs = jax.nn.softmax(scores, axis=-1).astype(jnp.bfloat16)
    context = jnp.einsum('bhl,bhld->bhd', attn_probs, cache_vals, preferred_element_type=jnp.float32)
    return context.astype(jnp.bfloat16)


def self_bias(rel_bias, positions, cache_len):
    distance = positions[:, None] - jnp.arange(cache_len)[None, :]
    pos_bias = jnp.take(rel_bias, jnp.clip(distance, 0, cache_len - 1), axis=1)
    pos_bias = jnp.where(distance[None] >= 0, pos_bias, NEG_BIG).transpose(1, 0, 2)
    return distance, pos_bias


def solution(mesh):
    ws_size = mesh.shape['ws']
    row_axes = ('dp', 'ws')
    row_vec = P(row_axes)
    row_mat = P(row_axes, None)
    cache_spec = P(row_axes, None, None, None)
    col_split = P(None, 'ws')
    in_specs = (row_mat, cache_spec, cache_spec, cache_spec, cache_spec, row_vec, row_mat, P(None, None), row_vec,
                P(None), P(None), P(None), col_split, col_split, col_split, col_split, col_split, col_split,
                col_split, P(None, None, 'ws'), P(None, 'ws', None))
    out_specs = (row_mat, cache_spec, cache_spec)

    def decoder_block(hidden, self_k, self_v, cross_k, cross_v, positions, enc_mask, rel_bias, expert_idx,
                      ln_self, ln_cross, ln_ffn, wq_self, wk_self, wv_self, wo_self, wq_cross, wo_cross,
                      w_router, w_in, w_out):
        gather_ws = functools.partial(lax.all_gather, axis_name='ws', tiled=True)
        wq_full = gather_ws(wq_self, axis=1)
        wk_full = gather_ws(wk_self, axis=1)
        wv_full = gather_ws(wv_self, axis=1)
        wo_full = gather_ws(wo_self, axis=1)
        wqc_full = gather_ws(wq_cross, axis=1)
        woc_full = gather_ws(wo_cross, axis=1)
        router_full = gather_ws(w_router, axis=1)
        win_full = gather_ws(w_in, axis=2)
        wout_full = gather_ws(w_out, axis=1)
        idx_all = gather_ws(expert_idx, axis=0)

        local_rows = hidden.shape[0]
        num_heads = rel_bias.shape[0]
        head_shape = (local_rows, num_heads, wq_full.shape[1] // num_heads)
        experts = win_full.shape[0]
        group_rows = local_rows * ws_size
        capacity = (2 * group_rows + experts - 1) // experts

        x_norm = rms_norm(hidden, ln_self)
        queries = project(x_norm, wq_full).reshape(head_shape)
        k_new = project(x_norm, wk_full).reshape(head_shape)
        v_new = project(x_norm, wv_full).reshape(head_shape)
        distance, pos_bias = self_bias(rel_bias, positions, self_k.shape[2])
        write_mask = (distance == 0)[:, None, :, None]
        new_self_k = jnp.where(write_mask, k_new[:, :, None, :], self_k)
        new_self_v = jnp.where(write_mask, v_new[:, :, None, :], self_v)
        context = attend(queries, new_self_k, new_self_v, pos_bias).reshape(local_rows, -1)
        after_self = (hidden.astype(jnp.float32) + jnp.dot(context, wo_full, preferred_element_type=jnp.float32)).astype(jnp.bfloat16)

        x_norm = rms_norm(after_self, ln_cross)
        queries = project(x_norm, wqc_full).reshape(head_shape)
        mask_bias = jnp.where(enc_mask == 1, 0.0, NEG_BIG)[:, None, :]
        context = attend(queries, cross_k, cross_v, mask_bias).reshape(local_rows, -1)
        after_cross = (after_self.astype(jnp.float32) + jnp.dot(context, woc_full, preferred_element_type=jnp.float32)).astype(jnp.bfloat16)

        x_norm = rms_norm(after_cross, ln_ffn)
        logits = jnp.dot(x_norm.astype(jnp.float32), router_full, precision=lax.Precision.HIGHEST,
                         preferred_element_type=jnp.float32)
        router_probs = jax.nn.softmax(logits, axis=-1)
        chosen = jnp.arange(experts)[None, :] == expert_idx[:, None]
        gate_val = jnp.sum(jnp.where(chosen, router_probs, 0.0), axis=-1)
        row_ids = lax.axis_index('ws') * local_rows + jnp.arange(local_rows)
        earlier = (idx_all[None, :] == expert_idx[:, None]) & (jnp.arange(group_rows)[None, :] < row_ids[:, None])
        slot_idx = jnp.sum(earlier.astype(jnp.int32), axis=1)
        keep_gate = jnp.where(slot_idx < capacity, gate_val, 0.0)
        ffn_hidden = jnp.einsum('bd,bdf->bf', x_norm, jnp.take(win_full, expert_idx, axis=0),
                                preferred_element_type=jnp.float32)
        ffn_hidden = jax.nn.relu(ffn_hidden).astype(jnp.bfloat16)
        expert_out = jnp.einsum('bf,bfd->bd', ffn_hidden, jnp.take(wout_full, expert_idx, axis=0),
                                preferred_element_type=jnp.float32).astype(jnp.bfloat16)
        hidden_out = (after_cross.astype(jnp.float32) + expert_out.astype(jnp.float32) * keep_gate[:, None]).astype(jnp.bfloat16)
        return hidden_out, new_self_k, new_self_v

    return jax.shard_map(decoder_block, mesh=mesh, in_specs=in_specs, out_specs=out_specs, check_vma=False)
```

profile of v0, /device:TPU:0, one launch (start us, length us, event | category | flops | bytes accessed | tf_op | source)
XLA Modules:
  0.0 1097.2 jit_solution(676834257540416350)
XLA Ops:
  7.2 0.7 all-gather.12.cloned.1.call-update
  8.0 0.7 all-gather.14.cloned.1.call-update
  8.7 0.7 all-gather.10.cloned.1.call-update
  11.2 0.7 all-gather.22.cloned.1.call-update
  12.0 0.7 all-gather.24.cloned.1.call-update
  12.7 0.8 copy.27
  13.5 0.7 compare_select_fusion
  14.3 3.7 gather_fusion
  18.0 1.2 dynamic-slice
  19.9 0.9 dynamic-update-slice
  20.7 13.8 %all-reduce = s32[128]{0:T(128)S(1)} all-reduce(s32[128]{0:T(128)S(1)} %dynamic-update-slice), channel_id=1, replica_groups=mesh['dp'=2,'ws'=16] {'ws'}, use_global_device_ids=true, to_apply=%add | all-reduce | flops 128 | bytes 1024
  34.5 18.1 %all-gather = f32[16,1,768]{2,1,0:T(1,128)S(1)} all-gather(f32[1,1,768]{2,1,0:T(1,128)} %bitcast.73), channel_id=1, replica_groups=mesh['dp'=2,'ws'=16] {'ws'}, dimensions={0}, use_global_device_ids=true | all-gather | bytes 52224 | tf_op jit(solution)/shard_map/all_gather | solution.py:57
  52.6 0.7 compare_select_fusion.3
  53.3 0.8 fusion.43
  54.1 0.8 convert_reduce_fusion
  54.9 0.7 compare_and_fusion
  55.6 0.7 fusion.53
  56.4 0.7 compare_select_fusion.2
  57.1 1.8 convolution_convert_fusion.2
  58.9 32.2 %all-gather.14.cloned.1.call-done = bf16[768,768]{0,1:T(8,128)(2,1)} async-done(((bf16[768,48]{0,1:T(8,128)(2,1)}), bf16[768,768]{0,1:T(8,128)(2,1)}) %all-gather.14.cloned.1.call-update) | async-done | bytes 1179664 | tf_op jit(solution)/shard_map/all_gather | solution.py:53
  91.1 1.7 convolution_convert_fusion.1
  92.9 37.8 %all-gather.10.cloned.1.call-done = bf16[768,768]{0,1:T(8,128)(2,1)} async-done(((bf16[768,48]{0,1:T(8,128)(2,1)}), bf16[768,768]{0,1:T(8,128)(2,1)}) %all-gather.10.cloned.1.call-update) | async-done | bytes 1179664 | tf_op jit(solution)/shard_map/all_gather | solution.py:51
  130.7 1.7 convolution_convert_fusion.3
  132.6 5.0 broadcast_select_fusion
  137.6 1.7 copy-done
  140.1 1.7 fusion.22
  142.2 2.8 fusion.75
  145.1 25.1 %all-gather.16.cloned.1.call-done = bf16[768,768]{0,1:T(8,128)(2,1)} async-done(((bf16[768,48]{0,1:T(8,128)(2,1)}), bf16[768,768]{0,1:T(8,128)(2,1)}) %all-gather.16.cloned.1.call-update) | async-done | bytes 1179664 | tf_op jit(solution)/shard_map/all_gather | solution.py:54
  170.2 1.8 multiply_reduce_fusion.1
  172.1 37.6 %all-gather.18.cloned.1.call-done = bf16[768,768]{0,1:T(8,128)(2,1)} async-done(((bf16[768,48]{0,1:T(8,128)(2,1)}), bf16[768,768]{0,1:T(8,128)(2,1)}) %all-gather.18.cloned.1.call-update) | async-done | bytes 1179664 | tf_op jit(solution)/shard_map/all_gather | solution.py:55
  209.7 1.7 convolution_convert_fusion
  211.5 3.3 fusion.76
  215.0 4.1 fusion.33
  219.2 30.0 %all-gather.20.cloned.1.call-done = bf16[768,768]{0,1:T(8,128)(2,1)} async-done(((bf16[768,48]{0,1:T(8,128)(2,1)}), bf16[768,768]{0,1:T(8,128)(2,1)}) %all-gather.20.cloned.1.call-update) | async-done | bytes 1179664 | tf_op jit(solution)/shard_map/all_gather | solution.py:56
  249.2 1.8 multiply_reduce_fusion
  252.3 362.8 %all-gather.22.cloned.1.call-done = bf16[16,768,3072]{1,2,0:T(8,128)(2,1)} async-done(((bf16[16,768,192]{1,2,0:T(8,128)(2,1)}), bf16[16,768,3072]{1,2,0:T(8,128)(2,1)}) %all-gather.22.cloned.1.call-update) | async-done | bytes 75497488 | tf_op jit(solution)/shard_map/all_gather | solution.py:58
  615.2 49.4 %fusion.71 = (bf16[16,768,1024]{1,2,0:T(8,128)(2,1)}, bf16[16,768,1024]{1,2,0:T(8,128)(2,1)}, bf16[16,768,1024]{1,2,0:T(8,128)(2,1)}) fusion(bf16[16,768,3072]{1,2,0:T(8,128)(2,1)} %all-gather.22.cloned.1.call-done), kind=kLoop, calls=%fused_computation.114 | loop fusion | bytes 150994944 | tf_op jit(solution)/shard_map/jit(_take)/gather | solution.py:96
  664.6 14.5 %gather_fusion.1 = bf16[8,768,1024]{1,2,0:T(8,128)(2,1)} fusion(bf16[16,768,1024]{1,2,0:T(8,128)(2,1)} %get-tuple-element.3, s32[1024]{0:T(1024)S(1)} %pad_clamp_fusion.1), kind=kCustom, calls=%fused_computation.1 | custom fusion | bytes 25165856 | tf_op jit(solution)/shard_map/jit(_take)/gather | solution.py:96
  679.1 14.6 %gather_fusion.2 = bf16[8,768,1024]{1,2,0:T(8,128)(2,1)} fusion(bf16[16,768,1024]{1,2,0:T(8,128)(2,1)} %get-tuple-element.4, s32[1024]{0:T(1024)S(1)} %pad_clamp_fusion.1), kind=kCustom, calls=%fused_computation.2 | custom fusion | bytes 25165856 | tf_op jit(solution)/shard_map/jit(_take)/gather | solution.py:96
  693.7 14.5 %gather_fusion.3 = bf16[8,768,1024]{1,2,0:T(8,128)(2,1)} fusion(bf16[16,768,1024]{1,2,0:T(8,128)(2,1)} %get-tuple-element.5, s32[1024]{0:T(1024)S(1)} %pad_clamp_fusion.1), kind=kCustom, calls=%fused_computation.3 | custom fusion | bytes 25165856 | tf_op jit(solution)/shard_map/jit(_take)/gather | solution.py:96
  708.2 16.5 %fusion.4 = bf16[8,1,3072]{2,1,0:T(2,128)(2,1)S(1)} fusion(bf16[8,768,1024]{1,2,0:T(8,128)(2,1)} %gather_fusion.3, bf16[8,768,1024]{1,2,0:T(8,128)(2,1)} %gather_fusion.2, bf16[8,768,1024]{1,2,0:T(8,128)(2,1)} %gather_fusion.1, pred[8]{0:T(512)(128)(4,1)S(1)} %compare_and_fusion, bf16[8,768,1]{1,0,2:T(8,128)(2,1)S(1)} %fusion.67), kind=kOutput, calls=%fused_computation.12 | convolution fusion | flops 169869312 | bytes 37810184 | tf_op jit(solution)/shard_map/bd,bdf->bf/dot_general | solution.py:96
  724.7 257.5 %all-gather.24.cloned.1.call-done = bf16[16,3072,768]{2,1,0:T(8,128)(2,1)} async-done(((bf16[16,192,768]{2,1,0:T(8,128)(2,1)}), bf16[16,3072,768]{2,1,0:T(8,128)(2,1)}) %all-gather.24.cloned.1.call-update) | async-done | bytes 75497488 | tf_op jit(solution)/shard_map/all_gather | solution.py:59
  982.2 49.5 %fusion.72 = (bf16[16,1024,768]{2,1,0:T(8,128)(2,1)}, bf16[16,1024,768]{2,1,0:T(8,128)(2,1)}, bf16[16,1024,768]{2,1,0:T(8,128)(2,1)}) fusion(bf16[16,3072,768]{2,1,0:T(8,128)(2,1)} %all-gather.24.cloned.1.call-done), kind=kLoop, calls=%fused_computation.115 | loop fusion | bytes 150994944 | tf_op jit(solution)/shard_map/jit(_take)/gather | solution.py:99
  1031.8 14.6 %gather_fusion.4 = bf16[8,1024,768]{2,1,0:T(8,128)(2,1)} fusion(bf16[16,1024,768]{2,1,0:T(8,128)(2,1)} %get-tuple-element.6, s32[1024]{0:T(1024)S(1)} %pad_clamp_fusion.1), kind=kCustom, calls=%fused_computation.4 | custom fusion | bytes 25165856 | tf_op jit(solution)/shard_map/jit(_take)/gather | solution.py:99
  1046.3 14.5 %gather_fusion.5 = bf16[8,1024,768]{2,1,0:T(8,128)(2,1)} fusion(bf16[16,1024,768]{2,1,0:T(8,128)(2,1)} %get-tuple-element.7, s32[1024]{0:T(1024)S(1)} %pad_clamp_fusion.1), kind=kCustom, calls=%fused_computation.5 | custom fusion | bytes 25165856 | tf_op jit(solution)/shard_map/jit(_take)/gather | solution.py:99
  1060.8 14.8 %gather_fusion.6 = bf16[8,1024,768]{2,1,0:T(8,128)(2,1)} fusion(bf16[16,1024,768]{2,1,0:T(8,128)(2,1)} %get-tuple-element.8, s32[1024]{0:T(1024)S(1)} %pad_clamp_fusion.1), kind=kCustom, calls=%fused_computation.6 | custom fusion | bytes 25165856 | tf_op jit(solution)/shard_map/jit(_take)/gather | solution.py:99
  1075.6 14.1 %fusion.9 = bf16[8,1,768]{2,1,0:T(2,128)(2,1)S(1)} fusion(bf16[8,1024,768]{2,1,0:T(8,128)(2,1)} %gather_fusion.6, bf16[8,1024,768]{2,1,0:T(8,128)(2,1)} %gather_fusion.5, bf16[8,1024,768]{2,1,0:T(8,128)(2,1)} %gather_fusion.4, pred[8]{0:T(512)(128)(4,1)S(1)} %compare_and_fusion, bf16[8,3072,1]{1,0,2:T(8,128)(2,1)S(1)} %fusion.39), kind=kOutput, calls=%fused_computation.18 | convolution fusion | flops 169869312 | bytes 37810184 | tf_op jit(solution)/shard_map/bf,bfd->bd/dot_general | solution.py:99
  1089.7 0.7 add_convert_fusion
  (57 shorter events, 5.5 us)
Async XLA Ops:
  7.2 123.6 %copy-start.4 = (bf16[8,768]{1,0:T(8,128)(2,1)S(1)}, bf16[8,768]{1,0:T(8,128)(2,1)}, u32[]{:S(2)}) copy-start(bf16[8,768]{1,0:T(8,128)(2,1)} %param.21) | copy-start | bytes 36868
  7.2 123.6 %copy-start.5 = (f32[768]{0:T(1024)S(1)}, f32[768]{0:T(1024)}, u32[]{:S(2)}) copy-start(f32[768]{0:T(1024)} %param.30) | copy-start | bytes 9220
  7.2 125.4 %copy-start.1 = (bf16[8,12,192,64]{2,3,1,0:T(8,128)(2,1)S(1)}, bf16[8,12,192,64]{2,3,1,0:T(8,128)(2,1)}, u32[]{:S(2)}) copy-start(bf16[8,12,192,64]{2,3,1,0:T(8,128)(2,1)} %param.23) | copy-start | bytes 7077892
  7.2 49.9 %all-gather.12.cloned.1.call-start = ((), (), s32[]{:S(2)}) async-start(), calls=%async_computation.1 | async-start | bytes 1253376 | tf_op jit(solution)/shard_map/all_gather | solution.py:52
  7.9 83.2 %all-gather.14.cloned.1.call-start = ((), (), s32[]{:S(2)}) async-start(), calls=%async_computation.2 | async-start | bytes 1253376 | tf_op jit(solution)/shard_map/all_gather | solution.py:53
  8.7 122.0 %all-gather.10.cloned.1.call-start = ((), (), s32[]{:S(2)}) async-start(), calls=%async_computation | async-start | bytes 1253376 | tf_op jit(solution)/shard_map/all_gather | solution.py:51
  9.4 160.8 %all-gather.16.cloned.1.call-start = ((), (), s32[]{:S(2)}) async-start(), calls=%async_computation.3 | async-start | bytes 1253376 | tf_op jit(solution)/shard_map/all_gather | solution.py:54
  10.0 199.7 %all-gather.18.cloned.1.call-start = ((), (), s32[]{:S(2)}) async-start(), calls=%async_computation.4 | async-start | bytes 1253376 | tf_op jit(solution)/shard_map/all_gather | solution.py:55
  10.6 238.6 %all-gather.20.cloned.1.call-start = ((), (), s32[]{:S(2)}) async-start(), calls=%async_computation.5 | async-start | bytes 1253376 | tf_op jit(solution)/shard_map/all_gather | solution.py:56
  11.2 604.0 %all-gather.22.cloned.1.call-start = ((), (), s32[]{:S(2)}) async-start(), calls=%async_computation.6 | async-start | bytes 80216064 | tf_op jit(solution)/shard_map/all_gather | solution.py:58
  11.9 970.3 %all-gather.24.cloned.1.call-start = ((), (), s32[]{:S(2)}) async-start(), calls=%async_computation.7 | async-start | bytes 80216064 | tf_op jit(solution)/shard_map/all_gather | solution.py:59
  132.6 77.1 %copy-start.7 = (f32[768]{0:T(1024)S(1)}, f32[768]{0:T(1024)}, u32[]{:S(2)}) copy-start(f32[768]{0:T(1024)} %param.31) | copy-start | bytes 9220
  137.6 1.7 copy-start
  140.1 111.0 %copy-start.6 = (f32[768]{0:T(1024)S(1)}, f32[768]{0:T(1024)}, u32[]{:S(2)}) copy-start(f32[768]{0:T(1024)} %param.32) | copy-start | bytes 9220
  140.1 111.5 %copy-start.8 = (s32[8]{0:T(128)S(1)}, s32[8]{0:T(128)}, u32[]{:S(2)}) copy-start(s32[8]{0:T(128)} %param.29) | copy-start | bytes 100
  251.0 1.3 copy-start.2
  1075.6 14.1 %copy-start.3 = (f32[8,768]{1,0:T(8,128)S(1)}, f32[8,768]{1,0:T(8,128)}, u32[]{:S(2)}) copy-start(f32[8,768]{1,0:T(8,128)} %copy-done.2) | copy-start | bytes 73732
  1075.6 14.1 %copy-start.9 = (f32[8]{0:T(128)S(1)}, f32[8]{0:T(128)}, u32[]{:S(2)}) copy-start(f32[8]{0:T(128)} %compare_select_fusion.4) | copy-start | bytes 100
Sparse Core Ops, SparseCore 0:
  10.3 41.2 all-gather.11
  53.9 37.1 all-gather.13
  93.4 37.3 all-gather.9
  132.9 37.3 all-gather.15
  172.3 37.3 all-gather.17
  211.8 37.3 all-gather.19
  250.7 364.4 all-gather.21
  616.7 365.4 all-gather.23
where the time goes:
time: 1100 us
  waiting for transfers between devices  788 us (72%)
  local copies, waits for them, and re-layouts  196 us (18%)
  matrix products  52 us (5%)
  blocking collectives  31.9 us (3%)
  between operations  15 us (1%)
  other arithmetic  13.8 us (1%)
    all_gather x1, waiting for transfers between devices, decoder_block(): win_full = gather_ws(w_in, axis=2)  363 us
    all_gather x1, waiting for transfers between devices, decoder_block(): wout_full = gather_ws(w_out, axis=1)  258 us
    gather x4, local copies, waits for them, and re-layouts, decoder_block(): jnp.take(wout_full, expert_idx, axis=0)  93.4 us
    gather x4, local copies, waits for them, and re-layouts, decoder_block(): jnp.take(win_full, expert_idx, axis=0)  93 us
    all_gather x1, waiting for transfers between devices, decoder_block(): wq_full = gather_ws(wq_self, axis=1)  37.8 us
    all_gather x1, waiting for transfers between devices, decoder_block(): wqc_full = gather_ws(wq_cross, axis=1)  37.6 us
    all_gather x1, waiting for transfers between devices, decoder_block(): wv_full = gather_ws(wv_self, axis=1)  32.2 us
    all_gather x1, waiting for transfers between devices, decoder_block(): woc_full = gather_ws(wo_cross, axis=1)  30 us
  transfers between devices with their start and end apart: 8, of which 7 were waited for; matrix products, arithmetic and copies ran while one was open for 14% of the time, Pallas kernels for 0%

commit v1 on v0

v1 whole, which is shorter than its diff:
```python
import jax
import jax.numpy as jnp
from jax import lax
from jax.experimental import pallas as pl
from jax.experimental.pallas import tpu as pltpu
from jax.sharding import PartitionSpec as P

EPS = 1e-6
NEG = -1e30
F32 = jnp.float32
BF16 = jnp.bfloat16
MESH = pl.DeviceIdType.MESH

ROWS = 8
D = 768
HEADS = 12
HPAD = 16
LS = 192
LC = 384
NDEV = 16
CB = 48
NT = (((1,), (1,)), ((), ()))

ALL_OFFS = [(kz, ky, kc) for kz in (2, 3, 1, 0) for ky in (1, 0) for kc in (1, 0) if (kz, ky, kc) != (0, 0, 0)]
SUB_OFFS = [(0, 1, 1), (0, 1, 0), (0, 0, 1)]
Z_OFFS = [(2, 0, 0), (3, 0, 0), (1, 0, 0)]


def dot_nt(a, b, **kw):
    return lax.dot_general(a, b, NT, preferred_element_type=F32, **kw)


def iota(shape, axis):
    return lax.broadcasted_iota(jnp.int32, shape, axis)


def rms(x, g):
    inv = lax.rsqrt(jnp.mean(x * x, axis=-1, keepdims=True) + EPS)
    return (x * inv * g).astype(BF16)


def head_mask():
    row = iota((HPAD, D), 0) * 64
    col = iota((HPAD, D), 1)
    return (col >= row) & (col < row + 64)


def attention(q8, k_ref, v_ref, bias_of, s_ref, ctx_ref):
    hm = head_mask()
    for b in range(ROWS):
        qb = jnp.where(hm, jnp.broadcast_to(q8[b:b + 1, :], (HPAD, D)), 0.0).astype(BF16)
        s_ref[b] = jnp.dot(qb, k_ref[b], preferred_element_type=F32) + bias_of(b)
    s = s_ref[...]
    p = jnp.exp(s - jnp.max(s, axis=-1, keepdims=True))
    s_ref[...] = p / jnp.sum(p, axis=-1, keepdims=True)
    for b in range(ROWS):
        cb = dot_nt(s_ref[b].astype(BF16), v_ref[b])
        ctx_ref[b:b + 1, :] = jnp.sum(jnp.where(hm, cb, 0.0), axis=0, keepdims=True)


def kernel(hid, kT, vT, ckT, cvT, pos_s, mask, rel, idx_s, ln1, ln2, ln3, wq, wk, wv, wo, wqc, woc, wr, win, wout,
           out_h, out_k, out_v,
           ck_v, cv_v, win_v, wout_v, mask_v, rel_v, ln_v, wqkv, m1, st2, r2, wgo, wgq, wgc, rw,
           c3, r4, st5, r5, c6, r7, st8, r8, bias_s, s_self, s_cross, ctx_v, h2_v, x3_v, u_v, k_v, v_v,
           ld, snd, rcv):
    me = lax.axis_index('ws')
    z = me // 4
    s = me % 4
    y = s // 2
    c = s % 2

    def peer_of(off):
        kz, ky, kc = off
        return ((z + kz) % 4) * 4 + ((y + ky) % 2) * 2 + (c + kc) % 2

    def send(src, dst, ph, off):
        pltpu.make_async_remote_copy(src_ref=src, dst_ref=dst, send_sem=snd.at[ph], recv_sem=rcv.at[ph],
                                     device_id={'ws': peer_of(off)}, device_id_type=MESH).start()

    def desc(buf, ph):
        return pltpu.make_async_remote_copy(src_ref=buf, dst_ref=buf, send_sem=snd.at[ph], recv_sem=rcv.at[ph],
                                            device_id={'ws': me}, device_id_type=MESH)

    bar = pltpu.get_barrier_semaphore()
    for off in ALL_OFFS:
        pl.semaphore_signal(bar, inc=1, device_id={'ws': peer_of(off)}, device_id_type=MESH)

    loads = {}

    def load(name, src, dst):
        cp = pltpu.make_async_copy(src, dst, ld.at[len(loads)])
        cp.start()
        loads[name] = cp

    load('hid', hid, m1.at[me, :, pl.ds(0, D)])
    load('wq', wq, wqkv.at[pl.ds(0, CB)])
    load('wk', wk, wqkv.at[pl.ds(CB, CB)])
    load('wv', wv, wqkv.at[pl.ds(2 * CB, CB)])
    load('ln1', ln1, ln_v.at[0])
    load('ln2', ln2, ln_v.at[1])
    load('ln3', ln3, ln_v.at[2])
    load('rel', rel, rel_v)
    load('mask', mask, mask_v)
    load('wr', wr, rw.at[me])
    load('wo', wo, wgo.at[z])
    load('wqc', wqc, wgq.at[z])
    load('woc', woc, wgc.at[z])
    load('k', kT, k_v)
    load('v', vT, v_v)
    load('ck', ckT, ck_v)
    load('cv', cvT, cv_v)
    load('win', win, win_v)
    load('wout', wout, wout_v)

    row8 = iota((ROWS, 128), 0)
    idx_own = jnp.zeros((ROWS, 128), jnp.int32)
    for i in range(ROWS):
        idx_own = jnp.where(row8 == i, idx_s[i], idx_own)
    idx_own = idx_own.astype(F32)
    m1[me, :, D:D + 128] = idx_own.astype(BF16)
    wqkv[3 * CB:256, :] = jnp.zeros((256 - 3 * CB, D), BF16)
    loads['hid'].wait()
    pl.semaphore_wait(bar, NDEV - 1)

    for off in ALL_OFFS:
        send(m1.at[me], m1.at[me], 0, off)

    loads['rel'].wait()
    loads['mask'].wait()
    rel_f = rel_v[...]
    rel_hi = rel_f.astype(BF16)
    rem = rel_f - rel_hi.astype(F32)
    rel_mid = rem.astype(BF16)
    rel_lo = (rem - rel_mid.astype(F32)).astype(BF16)
    src_i = iota((LS, LS), 0)
    dst_i = iota((LS, LS), 1)
    lane12 = iota((HEADS, LS), 1)
    bias_s[...] = jnp.zeros((ROWS, HPAD, LS), F32)
    for b in range(ROWS):
        pick = jnp.where(src_i + dst_i == pos_s[b], 1.0, 0.0).astype(BF16)
        bb = jnp.dot(rel_hi, pick, preferred_element_type=F32)
        bb = bb + jnp.dot(rel_mid, pick, preferred_element_type=F32)
        bb = bb + jnp.dot(rel_lo, pick, preferred_element_type=F32)
        bias_s[b, 0:HEADS, :] = jnp.where(lane12 <= pos_s[b], bb, NEG)
    for name in ('wq', 'wk', 'wv', 'ln1', 'ln2', 'ln3', 'wr', 'wo', 'wqc', 'woc'):
        loads[name].wait()

    desc(m1.at[pl.ds(0, NDEV - 1)], 0).wait_recv()
    hall = m1[:, :, 0:D].astype(F32).reshape(NDEV * ROWS, D)
    xn = rms(hall, ln_v[0])
    st2[...] = dot_nt(xn, wqkv[...]).reshape(NDEV, ROWS, 256).astype(BF16)
    r2[me] = st2[me]
    for off in ALL_OFFS:
        send(st2.at[peer_of(off)], r2.at[me], 1, off)
    for i, w in enumerate((wgo, wgq, wgc)):
        for off in Z_OFFS:
            send(w.at[z], w.at[z], 8 + i, off)
    for off in ALL_OFFS:
        send(rw.at[me], rw.at[me], 11, off)

    sel_r = iota((4 * CB, D), 0)
    sel_q = ((sel_r >= CB).astype(jnp.int32) + (sel_r >= 2 * CB).astype(jnp.int32)
             + (sel_r >= 3 * CB).astype(jnp.int32))
    sel = (iota((4 * CB, D), 1) == sel_r + sel_q * (4 * CB - CB) + s * CB)
    sel = jnp.where(sel, 1.0, 0.0).astype(BF16)
    h_sub = m1[pl.ds(4 * z, 4), :, 0:D].astype(F32).reshape(4 * ROWS, D).astype(BF16)
    h_blk = dot_nt(h_sub, sel)

    idx_all = m1[:, :, D:D + 128].astype(F32).reshape(NDEV * ROWS, 128)
    idx_t = idx_all.T
    earlier = (idx_t[0:ROWS, :] == idx_own) & (iota((ROWS, 128), 1) < me * ROWS + row8)
    slot = jnp.sum(jnp.where(earlier, 1.0, 0.0), axis=-1, keepdims=True)

    loads['k'].wait()
    loads['v'].wait()
    desc(r2.at[pl.ds(0, NDEV - 1)], 1).wait_recv()
    rv = r2[...].astype(F32)

    def columns(lo):
        return jnp.concatenate([rv[d, :, lo:lo + CB] for d in range(NDEV)], axis=-1)

    q8 = columns(0)
    k_cols = columns(CB).T
    v_cols = columns(2 * CB).T
    lane_s = iota((D, LS), 1)
    for b in range(ROWS):
        hit = lane_s == pos_s[b]
        k_v[b] = jnp.where(hit, jnp.broadcast_to(k_cols[:, b:b + 1], (D, LS)), k_v[b].astype(F32)).astype(BF16)
        v_v[b] = jnp.where(hit, jnp.broadcast_to(v_cols[:, b:b + 1], (D, LS)), v_v[b].astype(F32)).astype(BF16)
    st_k = pltpu.make_async_copy(k_v, out_k, ld.at[0])
    st_v = pltpu.make_async_copy(v_v, out_v, ld.at[1])
    st_k.start()
    st_v.start()
    attention(q8, k_v, v_v, lambda b: bias_s[b], s_self, ctx_v)

    def subgroup(buf, ph):
        for off in SUB_OFFS:
            send(buf.at[s], buf.at[s], ph, off)

    def natural(pieces):
        return jnp.concatenate([pieces[t][:, q * CB:(q + 1) * CB] for q in range(4) for t in range(4)], axis=-1)

    c3[s] = ctx_v[...].astype(BF16)
    subgroup(c3, 2)
    desc(wgo.at[pl.ds(0, 3)], 8).wait_recv()
    desc(c3.at[pl.ds(0, 3)], 2).wait_recv()
    ctx = c3[...].astype(F32).reshape(4 * ROWS, D).astype(BF16)
    h1_blk = (h_blk + dot_nt(ctx, wgo[...].reshape(4 * CB, D))).astype(BF16)
    r4[s, :, 0:4 * CB] = h1_blk
    subgroup(r4, 3)
    desc(wgq.at[pl.ds(0, 3)], 9).wait_recv()
    desc(r4.at[pl.ds(0, 3)], 3).wait_recv()
    r4f = r4[...].astype(F32)
    h1 = natural([r4f[t] for t in range(4)])
    x2 = rms(h1, ln_v[1])
    st5[:, :, 0:4 * CB] = dot_nt(x2, wgq[...].reshape(4 * CB, D)).reshape(4, ROWS, 4 * CB).astype(BF16)
    r5[s] = st5[s]
    for off in SUB_OFFS:
        kz, ky, kc = off
        send(st5.at[((y + ky) % 2) * 2 + (c + kc) % 2], r5.at[s], 4, off)
    loads['ck'].wait()
    loads['cv'].wait()
    desc(r5.at[pl.ds(0, 3)], 4).wait_recv()
    r5f = r5[...].astype(F32)
    q2 = natural([r5f[t] for t in range(4)])
    attention(q2, ck_v, cv_v, lambda b: jnp.where(mask_v[b:b + 1, :] == 1, 0.0, NEG), s_cross, ctx_v)

    c6[s] = ctx_v[...].astype(BF16)
    subgroup(c6, 5)
    desc(wgc.at[pl.ds(0, 3)], 10).wait_recv()
    desc(c6.at[pl.ds(0, 3)], 5).wait_recv()
    ctx2 = c6[...].astype(F32).reshape(4 * ROWS, D).astype(BF16)
    h2_blk = (h1_blk.astype(F32) + dot_nt(ctx2, wgc[...].reshape(4 * CB, D))).astype(BF16)
    r7[me, :, 0:4 * CB] = h2_blk
    for off in ALL_OFFS:
        send(r7.at[me], r7.at[me], 6, off)
    loads['win'].wait()
    loads['wout'].wait()
    desc(r7.at[pl.ds(0, NDEV - 1)], 6).wait_recv()
    for t in range(4):
        h2g = natural([r7[4 * t + u].astype(F32) for u in range(4)])
        h2_v[32 * t:32 * t + 32, :] = h2g
        x3_v[32 * t:32 * t + 32, :] = rms(h2g, ln_v[2]).astype(F32)
    x3 = x3_v[...].astype(BF16)
    idx3 = jnp.concatenate([idx_all, idx_all, idx_all], axis=-1)
    half = (iota((NDEV * ROWS, 384), 1) >= 192).astype(F32)
    for p in range(8):
        hh = dot_nt(x3, win_v[2 * p:2 * p + 2].reshape(384, D))
        u_v[:, 384 * p:384 * p + 384] = jnp.where(idx3 == half + float(2 * p), jnp.maximum(hh, 0.0), 0.0).astype(BF16)
    for n in range(3):
        yn = jnp.dot(u_v[...], wout_v[:, :, 256 * n:256 * n + 256].reshape(NDEV * 192, 256),
                     preferred_element_type=F32)
        st8[:, :, 256 * n:256 * n + 256] = yn.reshape(NDEV, ROWS, 256)
    for off in ALL_OFFS:
        send(st8.at[peer_of(off)], r8.at[me], 7, off)
    r8[me] = st8[me]

    desc(rw.at[pl.ds(0, NDEV - 1)], 11).wait_recv()
    x3_own = x3_v[pl.ds(pl.multiple_of(me * ROWS, ROWS), ROWS), :]
    h2_own = h2_v[pl.ds(pl.multiple_of(me * ROWS, ROWS), ROWS), :]
    logits = dot_nt(x3_own, rw[...].reshape(NDEV, D), precision=lax.Precision.HIGHEST)
    ex = jnp.exp(logits - jnp.max(logits, axis=-1, keepdims=True))
    probs = ex / jnp.sum(ex, axis=-1, keepdims=True)
    mine = iota((ROWS, NDEV), 1).astype(F32) == idx_own[:, 0:NDEV]
    gate = jnp.sum(jnp.where(mine, probs, 0.0), axis=-1, keepdims=True)
    gate = jnp.where(slot < float(NDEV), gate, 0.0)

    desc(r8.at[pl.ds(0, NDEV - 1)], 7).wait_recv()
    yv = jnp.sum(r8[...], axis=0).astype(BF16).astype(F32)
    out_h[...] = (h2_own + yv * gate).astype(BF16)

    st_k.wait()
    st_v.wait()
    for buf, ph in ((m1, 0), (st2, 1), (r7, 6), (st8, 7), (rw, 11)):
        desc(buf.at[pl.ds(0, NDEV - 1)], ph).wait_send()
    for buf, ph in ((c3, 2), (r4, 3), (st5, 4), (c6, 5), (wgo, 8), (wgq, 9), (wgc, 10)):
        desc(buf.at[pl.ds(0, 3)], ph).wait_send()


def solution(mesh):
    rows = ('dp', 'ws')
    row_vec = P(rows)
    row_mat = P(rows, None)
    cache = P(rows, None, None, None)
    col = P(None, 'ws')
    in_specs = (row_mat, cache, cache, cache, cache, row_vec, row_mat, P(None, None), row_vec,
                P(None), P(None), P(None), col, col, col, col, col, col,
                col, P(None, None, 'ws'), P(None, 'ws', None))
    out_specs = (row_mat, cache, cache)

    any_spec = pl.BlockSpec(memory_space=pl.ANY)
    smem = pl.BlockSpec(memory_space=pltpu.SMEM)
    vmem = pl.BlockSpec(memory_space=pltpu.VMEM)

    def block(hidden, self_k, self_v, cross_k, cross_v, positions, enc_mask, rel_bias, expert_idx,
              ln_self, ln_cross, ln_ffn, wq_self, wk_self, wv_self, wo_self, wq_cross, wo_cross,
              w_router, w_in, w_out):
        def flat(cache_arr):
            return jnp.swapaxes(cache_arr, 2, 3).reshape(ROWS, D, cache_arr.shape[2])

        def unflat(arr):
            return jnp.swapaxes(arr.reshape(ROWS, HEADS, 64, LS), 2, 3)

        args = (hidden, flat(self_k), flat(self_v), flat(cross_k), flat(cross_v), positions, enc_mask, rel_bias,
                expert_idx, ln_self.reshape(1, D), ln_cross.reshape(1, D), ln_ffn.reshape(1, D),
                wq_self.T, wk_self.T, wv_self.T, wo_self.T, wq_cross.T, wo_cross.T, w_router.T,
                jnp.swapaxes(w_in, 1, 2), w_out)
        specs = [any_spec] * len(args)
        specs[5] = smem
        specs[8] = smem
        V = pltpu.VMEM
        scratch = [
            V((ROWS, D, LC), BF16), V((ROWS, D, LC), BF16), V((NDEV, 192, D), BF16), V((NDEV, 192, D), BF16),
            V((ROWS, LC), jnp.int32), V((HEADS, LS), F32), V((3, 1, D), F32), V((256, D), BF16),
            V((NDEV, ROWS, D + 128), BF16), V((NDEV, ROWS, 256), BF16), V((NDEV, ROWS, 256), BF16),
            V((4, CB, D), BF16), V((4, CB, D), BF16), V((4, CB, D), BF16), V((NDEV, 1, D), F32),
            V((4, ROWS, D), BF16), V((4, 4 * ROWS, 256), BF16), V((4, ROWS, 256), BF16), V((4, ROWS, 256), BF16),
            V((4, ROWS, D), BF16), V((NDEV, 4 * ROWS, 256), BF16), V((NDEV, ROWS, D), F32), V((NDEV, ROWS, D), F32),
            V((ROWS, HPAD, LS), F32), V((ROWS, HPAD, LS), F32), V((ROWS, HPAD, LC), F32), V((ROWS, D), F32),
            V((NDEV * ROWS, D), F32), V((NDEV * ROWS, D), F32), V((NDEV * ROWS, NDEV * 192), BF16),
            V((ROWS, D, LS), BF16), V((ROWS, D, LS), BF16),
            pltpu.SemaphoreType.DMA((19,)), pltpu.SemaphoreType.DMA((12,)), pltpu.SemaphoreType.DMA((12,)),
        ]
        h_out, k_out, v_out = pl.pallas_call(
            kernel,
            out_shape=(jax.ShapeDtypeStruct((ROWS, D), BF16), jax.ShapeDtypeStruct((ROWS, D, LS), BF16),
                       jax.ShapeDtypeStruct((ROWS, D, LS), BF16)),
            in_specs=specs,
            out_specs=(vmem, any_spec, any_spec),
            scratch_shapes=scratch,
            compiler_params=pltpu.CompilerParams(collective_id=0, has_side_effects=True,
                                                 vmem_limit_bytes=60 * 1024 * 1024),
        )(*args)
        return h_out, unflat(k_out), unflat(v_out)

    return jax.shard_map(block, mesh=mesh, in_specs=in_specs, out_specs=out_specs, check_vma=False)
```

time: 1100 us -> 72.5 us (0.07)
  waiting for transfers between devices: 788 us -> 0 us
  local copies, waits for them, and re-layouts: 196 us -> 10.9 us
  Pallas kernels: 0 us -> 60.5 us
  matrix products: 52 us -> 0 us
  blocking collectives: 31.9 us -> 0 us
  between operations: 15 us -> 0.64 us
  other arithmetic: 13.8 us -> 0 us
    all_gather x8 -> x0, waiting for transfers between devices: 783 us -> none  [the longest x1 363 us: decoder_block(): win_full = gather_ws(w_in, axis=2)]
    gather x9 -> x0, local copies, waits for them, and re-layouts: 190 us -> none  [the longest x4 93.4 us: decoder_block(): jnp.take(wout_full, expert_idx, axis=0)]
    pallas_call x0 -> x1, Pallas kernels: none -> 60.5 us  [block(): pl.pallas_call(kernel, out_shape=(jax.ShapeDtypeStruct((ROWS, D), BF16),...]
    dot_general x13 -> x0, matrix products: 52 us -> none  [the longest x1 16.5 us: decoder_block(): jnp.einsum('bd,bdf->bf', x_norm, jnp.take(win_full, expert_idx, axis=0),...]
    all_gather x1 -> x0, blocking collectives: 18.1 us -> none  [decoder_block(): router_full = gather_ws(w_router, axis=1)]
    unnamed x1 -> x0, blocking collectives: 13.8 us -> none
  transfers between devices with their start and end apart: 8 -> 0, of which waited for: 7 -> 0; matrix products, arithmetic and copies ran while one was open for 14% -> 0% of each run, Pallas kernels for 0% -> 0%
where the time goes in v1:
time: 72.5 us; the launch traced here: 72 us
  Pallas kernels  60.5 us (83%)
  local copies, waits for them, and re-layouts  10.9 us (15%)
    pallas_call x1, Pallas kernels, block(): pl.pallas_call(kernel, out_shape=(jax.ShapeDtypeStruct((ROWS, D), BF16),...  60.5 us
    unnamed x5, local copies, waits for them, and re-layouts  7.09 us

profile of v1, /device:TPU:0, one launch (start us, length us, event | category | flops | bytes accessed | tf_op | source)
XLA Modules:
  0.0 72.0 jit_solution(8698473841199371695)
XLA Ops:
  0.6 1.3 %reshape.37.ln1 = f32[1,768]{1,0:T(1,128)} reshape(f32[768]{0:T(1024)} %param.30) | data formatting | bytes 6144 | tf_op jit(solution)/shard_map/reshape | solution.py:305
  1.9 1.3 %reshape.38.ln2 = f32[1,768]{1,0:T(1,128)} reshape(f32[768]{0:T(1024)} %param.31) | data formatting | bytes 6144 | tf_op jit(solution)/shard_map/reshape | solution.py:305
  3.2 1.3 %reshape.39.ln3 = f32[1,768]{1,0:T(1,128)} reshape(f32[768]{0:T(1024)} %param.32) | data formatting | bytes 6144 | tf_op jit(solution)/shard_map/reshape | solution.py:305
  4.4 60.5 %shard_map.220 = (bf16[8,768]{1,0:T(8,128)(2,1)}, bf16[8,768,192]{2,1,0:T(8,128)(2,1)}, bf16[8,768,192]{2,1,0:T(8,128)(2,1)}) custom-call(bf16[8,768]{1,0:T(8,128)(2,1)} %hid.1, bf16[8,768,192]{2,1,0:T(8,128)(2,1)} %bitcast.31, bf16[8,768,192]{2,1,0:T(8,128)(2,1)} %bitcast.32, bf16[8,768,384]{2,1,0:T(8,128)(2,1)} %bitcast.26, bf16[8,768,384]{2,1,0:T(8,128)(2,1)} %bitcast.27, ...), custom_call_target="tpu_custom_call" | custom-call | tf_op jit(solution)/shard_map/pallas_call | solution.py:324
  64.9 1.3 %copy.27 = bf16[8,768]{1,0:T(8,128)(2,1)} copy(bf16[8,768]{1,0:T(8,128)(2,1)} %get-tuple-element.12) | data formatting | bytes 24576
  66.2 0.0 copy-start
  66.2 4.1 %copy.28 = bf16[8,12,192,64]{2,3,1,0:T(8,128)(2,1)} copy(bf16[8,12,192,64]{2,3,1,0:T(8,128)(2,1)} %bitcast.30) | data formatting | bytes 4718592
  70.4 0.0 copy-done
  70.4 1.7 %copy.29 = bf16[8,12,192,64]{2,3,1,0:T(8,128)(2,1)} copy(bf16[8,12,192,64]{2,3,1,0:T(8,128)(2,1)S(1)} %bitcast.29) | data formatting | bytes 4718592
Async XLA Ops:
  66.2 4.1 %copy-start = (bf16[8,768,192]{2,1,0:T(8,128)(2,1)S(1)}, bf16[8,768,192]{2,1,0:T(8,128)(2,1)}, u32[]{:S(2)}) copy-start(bf16[8,768,192]{2,1,0:T(8,128)(2,1)} %get-tuple-element.8) | copy-start | bytes 7077892

commit v2 on v1

--- a/solution.py
+++ b/solution.py
@@ -22,6 +22,7 @@
 NT = (((1,), (1,)), ((), ()))
 
 ALL_OFFS = [(kz, ky, kc) for kz in (2, 3, 1, 0) for ky in (1, 0) for kc in (1, 0) if (kz, ky, kc) != (0, 0, 0)]
+CHIP_OFFS = [off for off in ALL_OFFS if off[2] == 0]
 SUB_OFFS = [(0, 1, 1), (0, 1, 0), (0, 0, 1)]
 Z_OFFS = [(2, 0, 0), (3, 0, 0), (1, 0, 0)]
 
@@ -59,9 +60,9 @@
 
 
 def kernel(hid, kT, vT, ckT, cvT, pos_s, mask, rel, idx_s, ln1, ln2, ln3, wq, wk, wv, wo, wqc, woc, wr, win, wout,
-           out_h, out_k, out_v,
-           ck_v, cv_v, win_v, wout_v, mask_v, rel_v, ln_v, wqkv, m1, st2, r2, wgo, wgq, wgc, rw,
-           c3, r4, st5, r5, c6, r7, st8, r8, bias_s, s_self, s_cross, ctx_v, h2_v, x3_v, u_v, k_v, v_v,
+           out_h, k_v, v_v,
+           ck_v, cv_v, win_v, wout_v, mask_v, rel_v, ln1_v, ln2_v, ln3_v, wqkv, m1, ix, st2, r2, wgo, wgq, wgc, rw,
+           c3, r4, st5, r5, c6, r7, st8, r8, st9, r9, bias_s, s_self, s_cross, ctx_v, h2_v, x3_v, u_v,
            ld, snd, rcv):
     me = lax.axis_index('ws')
     z = me // 4
@@ -92,13 +93,13 @@
         cp.start()
         loads[name] = cp
 
-    load('hid', hid, m1.at[me, :, pl.ds(0, D)])
+    load('hid', hid, m1.at[me])
     load('wq', wq, wqkv.at[pl.ds(0, CB)])
     load('wk', wk, wqkv.at[pl.ds(CB, CB)])
     load('wv', wv, wqkv.at[pl.ds(2 * CB, CB)])
-    load('ln1', ln1, ln_v.at[0])
-    load('ln2', ln2, ln_v.at[1])
-    load('ln3', ln3, ln_v.at[2])
+    load('ln1', ln1, ln1_v)
+    load('ln2', ln2, ln2_v)
+    load('ln3', ln3, ln3_v)
     load('rel', rel, rel_v)
     load('mask', mask, mask_v)
     load('wr', wr, rw.at[me])
@@ -117,13 +118,16 @@
     for i in range(ROWS):
         idx_own = jnp.where(row8 == i, idx_s[i], idx_own)
     idx_own = idx_own.astype(F32)
-    m1[me, :, D:D + 128] = idx_own.astype(BF16)
+    ix[me] = idx_own.astype(BF16)
     wqkv[3 * CB:256, :] = jnp.zeros((256 - 3 * CB, D), BF16)
     loads['hid'].wait()
     pl.semaphore_wait(bar, NDEV - 1)
 
     for off in ALL_OFFS:
         send(m1.at[me], m1.at[me], 0, off)
+    loads['wo'].wait()
+    for off in Z_OFFS:
+        send(wgo.at[z], wgo.at[z], 8, off)
 
     loads['rel'].wait()
     loads['mask'].wait()
@@ -142,20 +146,21 @@
         bb = bb + jnp.dot(rel_mid, pick, preferred_element_type=F32)
         bb = bb + jnp.dot(rel_lo, pick, preferred_element_type=F32)
         bias_s[b, 0:HEADS, :] = jnp.where(lane12 <= pos_s[b], bb, NEG)
-    for name in ('wq', 'wk', 'wv', 'ln1', 'ln2', 'ln3', 'wr', 'wo', 'wqc', 'woc'):
+    for name in ('wq', 'wk', 'wv', 'ln1', 'ln2', 'ln3', 'wr', 'wqc', 'woc'):
         loads[name].wait()
 
     desc(m1.at[pl.ds(0, NDEV - 1)], 0).wait_recv()
-    hall = m1[:, :, 0:D].astype(F32).reshape(NDEV * ROWS, D)
-    xn = rms(hall, ln_v[0])
+    hall = m1[...].astype(F32).reshape(NDEV * ROWS, D)
+    xn = rms(hall, ln1_v[...].reshape(1, D))
     st2[...] = dot_nt(xn, wqkv[...]).reshape(NDEV, ROWS, 256).astype(BF16)
     r2[me] = st2[me]
     for off in ALL_OFFS:
         send(st2.at[peer_of(off)], r2.at[me], 1, off)
-    for i, w in enumerate((wgo, wgq, wgc)):
+    for i, w in enumerate((wgq, wgc)):
         for off in Z_OFFS:
-            send(w.at[z], w.at[z], 8 + i, off)
-    for off in ALL_OFFS:
+            send(w.at[z], w.at[z], 9 + i, off)
+    for off in ALL_OFFS:
+        send(ix.at[me], ix.at[me], 12, off)
         send(rw.at[me], rw.at[me], 11, off)
 
     sel_r = iota((4 * CB, D), 0)
@@ -163,13 +168,8 @@
              + (sel_r >= 3 * CB).astype(jnp.int32))
     sel = (iota((4 * CB, D), 1) == sel_r + sel_q * (4 * CB - CB) + s * CB)
     sel = jnp.where(sel, 1.0, 0.0).astype(BF16)
-    h_sub = m1[pl.ds(4 * z, 4), :, 0:D].astype(F32).reshape(4 * ROWS, D).astype(BF16)
+    h_sub = m1[pl.ds(4 * z, 4)].astype(F32).reshape(4 * ROWS, D).astype(BF16)
     h_blk = dot_nt(h_sub, sel)
-
-    idx_all = m1[:, :, D:D + 128].astype(F32).reshape(NDEV * ROWS, 128)
-    idx_t = idx_all.T
-    earlier = (idx_t[0:ROWS, :] == idx_own) & (iota((ROWS, 128), 1) < me * ROWS + row8)
-    slot = jnp.sum(jnp.where(earlier, 1.0, 0.0), axis=-1, keepdims=True)
 
     loads['k'].wait()
     loads['v'].wait()
@@ -187,10 +187,6 @@
         hit = lane_s == pos_s[b]
         k_v[b] = jnp.where(hit, jnp.broadcast_to(k_cols[:, b:b + 1], (D, LS)), k_v[b].astype(F32)).astype(BF16)
         v_v[b] = jnp.where(hit, jnp.broadcast_to(v_cols[:, b:b + 1], (D, LS)), v_v[b].astype(F32)).astype(BF16)
-    st_k = pltpu.make_async_copy(k_v, out_k, ld.at[0])
-    st_v = pltpu.make_async_copy(v_v, out_v, ld.at[1])
-    st_k.start()
-    st_v.start()
     attention(q8, k_v, v_v, lambda b: bias_s[b], s_self, ctx_v)
 
     def subgroup(buf, ph):
@@ -199,6 +195,10 @@
 
     def natural(pieces):
         return jnp.concatenate([pieces[t][:, q * CB:(q + 1) * CB] for q in range(4) for t in range(4)], axis=-1)
+
+    def unpack(blk):
+        tail = jnp.concatenate([blk[32:48, 0:64], blk[32:48, 64:128]], axis=0)
+        return jnp.concatenate([blk[0:32, :], tail], axis=-1)
 
     c3[s] = ctx_v[...].astype(BF16)
     subgroup(c3, 2)
@@ -212,7 +212,7 @@
     desc(r4.at[pl.ds(0, 3)], 3).wait_recv()
     r4f = r4[...].astype(F32)
     h1 = natural([r4f[t] for t in range(4)])
-    x2 = rms(h1, ln_v[1])
+    x2 = rms(h1, ln2_v[...].reshape(1, D))
     st5[:, :, 0:4 * CB] = dot_nt(x2, wgq[...].reshape(4 * CB, D)).reshape(4, ROWS, 4 * CB).astype(BF16)
     r5[s] = st5[s]
     for off in SUB_OFFS:
@@ -231,29 +231,52 @@
     desc(c6.at[pl.ds(0, 3)], 5).wait_recv()
     ctx2 = c6[...].astype(F32).reshape(4 * ROWS, D).astype(BF16)
     h2_blk = (h1_blk.astype(F32) + dot_nt(ctx2, wgc[...].reshape(4 * CB, D))).astype(BF16)
-    r7[me, :, 0:4 * CB] = h2_blk
+    h2_f = h2_blk.astype(F32)
+    r7[me, 0:32, :] = h2_f[:, 0:128].astype(BF16)
+    r7[me, 32:48, :] = jnp.concatenate([h2_f[0:16, 128:192], h2_f[16:32, 128:192]], axis=-1).astype(BF16)
     for off in ALL_OFFS:
         send(r7.at[me], r7.at[me], 6, off)
+    desc(ix.at[pl.ds(0, NDEV - 1)], 12).wait_recv()
+    idx_all = ix[...].astype(F32).reshape(NDEV * ROWS, 128)
+    idx_t = idx_all.T
+    earlier = (idx_t[0:ROWS, :] == idx_own) & (iota((ROWS, 128), 1) < me * ROWS + row8)
+    slot = jnp.sum(jnp.where(earlier, 1.0, 0.0), axis=-1, keepdims=True)
     loads['win'].wait()
     loads['wout'].wait()
     desc(r7.at[pl.ds(0, NDEV - 1)], 6).wait_recv()
     for t in range(4):
-        h2g = natural([r7[4 * t + u].astype(F32) for u in range(4)])
+        h2g = natural([unpack(r7[4 * t + u].astype(F32)) for u in range(4)])
         h2_v[32 * t:32 * t + 32, :] = h2g
-        x3_v[32 * t:32 * t + 32, :] = rms(h2g, ln_v[2]).astype(F32)
+        x3_v[32 * t:32 * t + 32, :] = rms(h2g, ln3_v[...].reshape(1, D)).astype(F32)
     x3 = x3_v[...].astype(BF16)
     idx3 = jnp.concatenate([idx_all, idx_all, idx_all], axis=-1)
     half = (iota((NDEV * ROWS, 384), 1) >= 192).astype(F32)
     for p in range(8):
         hh = dot_nt(x3, win_v[2 * p:2 * p + 2].reshape(384, D))
         u_v[:, 384 * p:384 * p + 384] = jnp.where(idx3 == half + float(2 * p), jnp.maximum(hh, 0.0), 0.0).astype(BF16)
-    for n in range(3):
+    chip = me // 2
+    sibling = (0, 0, 1)
+
+    def partial(n):
         yn = jnp.dot(u_v[...], wout_v[:, :, 256 * n:256 * n + 256].reshape(NDEV * 192, 256),
-                     preferred_element_type=F32)
-        st8[:, :, 256 * n:256 * n + 256] = yn.reshape(NDEV, ROWS, 256)
-    for off in ALL_OFFS:
-        send(st8.at[peer_of(off)], r8.at[me], 7, off)
-    r8[me] = st8[me]
+                     preferred_element_type=F32).reshape(8, 2, ROWS, 256)
+        st8[n, 0] = yn[:, 0]
+        st8[n, 1] = yn[:, 1]
+        send(st8.at[n, 1 - c], r8.at[n], 13 + n, sibling)
+
+    def reduce_send(n):
+        desc(r8.at[n], 13 + n).wait_recv()
+        st9[n] = st8[n, c] + r8[n]
+        for off in CHIP_OFFS:
+            send(st9.at[n, peer_of(off) // 2], r9.at[n, chip], 16 + n, off)
+        r9[n, chip] = st9[n, chip]
+
+    partial(0)
+    partial(1)
+    reduce_send(0)
+    partial(2)
+    reduce_send(1)
+    reduce_send(2)
 
     desc(rw.at[pl.ds(0, NDEV - 1)], 11).wait_recv()
     x3_own = x3_v[pl.ds(pl.multiple_of(me * ROWS, ROWS), ROWS), :]
@@ -265,16 +288,27 @@
     gate = jnp.sum(jnp.where(mine, probs, 0.0), axis=-1, keepdims=True)
     gate = jnp.where(slot < float(NDEV), gate, 0.0)
 
-    desc(r8.at[pl.ds(0, NDEV - 1)], 7).wait_recv()
-    yv = jnp.sum(r8[...], axis=0).astype(BF16).astype(F32)
+    for n in range(3):
+        desc(r9.at[n, pl.ds(0, 7)], 16 + n).wait_recv()
+    yv = jnp.concatenate([jnp.sum(r9[n], axis=0) for n in range(3)], axis=-1).astype(BF16).astype(F32)
     out_h[...] = (h2_own + yv * gate).astype(BF16)
 
-    st_k.wait()
-    st_v.wait()
-    for buf, ph in ((m1, 0), (st2, 1), (r7, 6), (st8, 7), (rw, 11)):
+    for buf, ph in ((m1, 0), (st2, 1), (r7, 6), (rw, 11), (ix, 12)):
         desc(buf.at[pl.ds(0, NDEV - 1)], ph).wait_send()
+    for n in range(3):
+        desc(st9.at[n, pl.ds(0, 7)], 16 + n).wait_send()
+        desc(r8.at[n], 13 + n).wait_send()
     for buf, ph in ((c3, 2), (r4, 3), (st5, 4), (c6, 5), (wgo, 8), (wgq, 9), (wgc, 10)):
         desc(buf.at[pl.ds(0, 3)], ph).wait_send()
+
+
+def store(h_in, k_in, v_in, h_out, k_out, v_out, sem):
+    copies = [pltpu.make_async_copy(src, dst, sem.at[i])
+              for i, (src, dst) in enumerate(((k_in, k_out), (v_in, v_out), (h_in, h_out)))]
+    for cp in copies:
+        cp.start()
+    for cp in copies:
+        cp.wait()
 
 
 def solution(mesh):
@@ -288,7 +322,7 @@
                 col, P(None, None, 'ws'), P(None, 'ws', None))
     out_specs = (row_mat, cache, cache)
 
-    any_spec = pl.BlockSpec(memory_space=pl.ANY)
+    any_spec = pl.BlockSpec(memory_space=pltpu.HBM)
     smem = pl.BlockSpec(memory_space=pltpu.SMEM)
     vmem = pl.BlockSpec(memory_space=pltpu.VMEM)
 
@@ -302,7 +336,7 @@
             return jnp.swapaxes(arr.reshape(ROWS, HEADS, 64, LS), 2, 3)
 
         args = (hidden, flat(self_k), flat(self_v), flat(cross_k), flat(cross_v), positions, enc_mask, rel_bias,
-                expert_idx, ln_self.reshape(1, D), ln_cross.reshape(1, D), ln_ffn.reshape(1, D),
+                expert_idx, ln_self, ln_cross, ln_ffn,
                 wq_self.T, wk_self.T, wv_self.T, wo_self.T, wq_cross.T, wo_cross.T, w_router.T,
                 jnp.swapaxes(w_in, 1, 2), w_out)
         specs = [any_spec] * len(args)
@@ -311,26 +345,32 @@
         V = pltpu.VMEM
         scratch = [
             V((ROWS, D, LC), BF16), V((ROWS, D, LC), BF16), V((NDEV, 192, D), BF16), V((NDEV, 192, D), BF16),
-            V((ROWS, LC), jnp.int32), V((HEADS, LS), F32), V((3, 1, D), F32), V((256, D), BF16),
-            V((NDEV, ROWS, D + 128), BF16), V((NDEV, ROWS, 256), BF16), V((NDEV, ROWS, 256), BF16),
+            V((ROWS, LC), jnp.int32), V((HEADS, LS), F32), V((D,), F32), V((D,), F32), V((D,), F32), V((256, D), BF16),
+            V((NDEV, ROWS, D), BF16), V((NDEV, ROWS, 128), BF16), V((NDEV, ROWS, 256), BF16), V((NDEV, ROWS, 256), BF16),
             V((4, CB, D), BF16), V((4, CB, D), BF16), V((4, CB, D), BF16), V((NDEV, 1, D), F32),
             V((4, ROWS, D), BF16), V((4, 4 * ROWS, 256), BF16), V((4, ROWS, 256), BF16), V((4, ROWS, 256), BF16),
-            V((4, ROWS, D), BF16), V((NDEV, 4 * ROWS, 256), BF16), V((NDEV, ROWS, D), F32), V((NDEV, ROWS, D), F32),
+            V((4, ROWS, D), BF16), V((NDEV, CB, 128), BF16), V((3, 2, 8, ROWS, 256), F32), V((3, 8, ROWS, 256), F32),
+            V((3, 8, ROWS, 256), F32), V((3, 8, ROWS, 256), F32),
             V((ROWS, HPAD, LS), F32), V((ROWS, HPAD, LS), F32), V((ROWS, HPAD, LC), F32), V((ROWS, D), F32),
             V((NDEV * ROWS, D), F32), V((NDEV * ROWS, D), F32), V((NDEV * ROWS, NDEV * 192), BF16),
-            V((ROWS, D, LS), BF16), V((ROWS, D, LS), BF16),
-            pltpu.SemaphoreType.DMA((19,)), pltpu.SemaphoreType.DMA((12,)), pltpu.SemaphoreType.DMA((12,)),
+            pltpu.SemaphoreType.DMA((19,)), pltpu.SemaphoreType.DMA((19,)), pltpu.SemaphoreType.DMA((19,)),
         ]
         h_out, k_out, v_out = pl.pallas_call(
             kernel,
-            out_shape=(jax.ShapeDtypeStruct((ROWS, D), BF16), jax.ShapeDtypeStruct((ROWS, D, LS), BF16),
-                       jax.ShapeDtypeStruct((ROWS, D, LS), BF16)),
+            out_shape=(V((ROWS, D), BF16), V((ROWS, D, LS), BF16), V((ROWS, D, LS), BF16)),
             in_specs=specs,
-            out_specs=(vmem, any_spec, any_spec),
+            out_specs=(vmem, vmem, vmem),
             scratch_shapes=scratch,
             compiler_params=pltpu.CompilerParams(collective_id=0, has_side_effects=True,
-                                                 vmem_limit_bytes=60 * 1024 * 1024),
+                                                 vmem_limit_bytes=67043328 - 2 * 3145728 - 16384),
         )(*args)
+        outs = (jax.ShapeDtypeStruct((ROWS, D), BF16), jax.ShapeDtypeStruct((ROWS, D, LS), BF16),
+                jax.ShapeDtypeStruct((ROWS, D, LS), BF16))
+        h_out, k_out, v_out = pl.pallas_call(
+            store, out_shape=outs, in_specs=[vmem] * 3, out_specs=(any_spec,) * 3,
+            scratch_shapes=[pltpu.SemaphoreType.DMA((3,))],
+            compiler_params=pltpu.CompilerParams(vmem_limit_bytes=4 * 1024 * 1024),
+        )(h_out, k_out, v_out)
         return h_out, unflat(k_out), unflat(v_out)
 
     return jax.shard_map(block, mesh=mesh, in_specs=in_specs, out_specs=out_specs, check_vma=False)

time: 72.5 us -> 62.7 us (0.86)
  local copies, waits for them, and re-layouts: 10.9 us -> 0 us
  Pallas kernels: 60.5 us -> 61.8 us
    unnamed x5 -> x0, local copies, waits for them, and re-layouts: 7.09 us -> none
    reshape x3 -> x0, local copies, waits for them, and re-layouts: 3.8 us -> none  [the longest x1 1.27 us: block(): ln_self.reshape(1, D)]
    pallas_call x1 -> x2, Pallas kernels: 60.5 us -> 61.8 us  [the longest x1 59.1 us: block(): pl.pallas_call(kernel, out_shape=(V((ROWS, D), BF16), V((ROWS, D, LS), BF...]
where the time goes in v2:
time: 62.7 us; the launch traced here: 62.4 us
  Pallas kernels  61.8 us (99%)
  between operations  0.65 us (1%)
    pallas_call x1, Pallas kernels, block(): pl.pallas_call(kernel, out_shape=(V((ROWS, D), BF16), V((ROWS, D, LS), BF...  59.1 us
    pallas_call x1, Pallas kernels, block(): pl.pallas_call(store, out_shape=outs, in_specs=[vmem] * 3, out_specs=(any...  2.73 us

profile of v2, /device:TPU:0, one launch (start us, length us, event | category | flops | bytes accessed | tf_op | source)
XLA Modules:
  0.0 62.4 jit_solution(5970435983481879899)
XLA Ops:
  0.6 59.1 %shard_map.220 = (bf16[8,768]{1,0:T(8,128)(2,1)S(1)}, bf16[8,768,192]{2,1,0:T(8,128)(2,1)S(1)}, bf16[8,768,192]{2,1,0:T(8,128)(2,1)S(1)}) custom-call(bf16[8,768]{1,0:T(8,128)(2,1)} %hid.1, bf16[8,768,192]{2,1,0:T(8,128)(2,1)} %bitcast.29, bf16[8,768,192]{2,1,0:T(8,128)(2,1)} %bitcast.30, bf16[8,768,384]{2,1,0:T(8,128)(2,1)} %bitcast.26, ...), custom_call_target="tpu_custom_call" | custom-call | tf_op jit(solution)/shard_map/pallas_call | solution.py:358
  59.7 2.7 %shard_map.221 = (bf16[8,768]{1,0:T(8,128)(2,1)}, bf16[8,768,192]{2,1,0:T(8,128)(2,1)}, bf16[8,768,192]{2,1,0:T(8,128)(2,1)}) custom-call(bf16[8,768]{1,0:T(8,128)(2,1)S(1)} %get-tuple-element.9.h_in, bf16[8,768,192]{2,1,0:T(8,128)(2,1)S(1)} %get-tuple-element.10.k_in, bf16[8,768,192]{2,1,0:T(8,128)(2,1)S(1)} %get-tuple-element.11.v_in), custom_call_target="tpu_custom_call" | custom-call | tf_op jit(solution)/shard_map/pallas_call | solution.py:369

commit v3 on v2

--- a/solution.py
+++ b/solution.py
@@ -106,12 +106,6 @@
     load('wo', wo, wgo.at[z])
     load('wqc', wqc, wgq.at[z])
     load('woc', woc, wgc.at[z])
-    load('k', kT, k_v)
-    load('v', vT, v_v)
-    load('ck', ckT, ck_v)
-    load('cv', cvT, cv_v)
-    load('win', win, win_v)
-    load('wout', wout, wout_v)
 
     row8 = iota((ROWS, 128), 0)
     idx_own = jnp.zeros((ROWS, 128), jnp.int32)
@@ -128,6 +122,8 @@
     loads['wo'].wait()
     for off in Z_OFFS:
         send(wgo.at[z], wgo.at[z], 8, off)
+    load('k', kT, k_v)
+    load('v', vT, v_v)
 
     loads['rel'].wait()
     loads['mask'].wait()
@@ -162,6 +158,8 @@
     for off in ALL_OFFS:
         send(ix.at[me], ix.at[me], 12, off)
         send(rw.at[me], rw.at[me], 11, off)
+    load('ck', ckT, ck_v)
+    load('cv', cvT, cv_v)
 
     sel_r = iota((4 * CB, D), 0)
     sel_q = ((sel_r >= CB).astype(jnp.int32) + (sel_r >= 2 * CB).astype(jnp.int32)
@@ -202,6 +200,8 @@
 
     c3[s] = ctx_v[...].astype(BF16)
     subgroup(c3, 2)
+    load('win', win, win_v)
+    load('wout', wout, wout_v)
     desc(wgo.at[pl.ds(0, 3)], 8).wait_recv()
     desc(c3.at[pl.ds(0, 3)], 2).wait_recv()
     ctx = c3[...].astype(F32).reshape(4 * ROWS, D).astype(BF16)

time: 62.7 us -> 62.7 us (level)
  no operation moved by 1% of the time
where the time goes in v3:
time: 62.7 us; the launch traced here: 62.4 us
  Pallas kernels  61.8 us (99%)
  between operations  0.65 us (1%)
    pallas_call x1, Pallas kernels, block(): pl.pallas_call(kernel, out_shape=(V((ROWS, D), BF16), V((ROWS, D, LS), BF...  59 us
    pallas_call x1, Pallas kernels, block(): pl.pallas_call(store, out_shape=outs, in_specs=[vmem] * 3, out_specs=(any...  2.73 us

profile of v3, /device:TPU:0, one launch (start us, length us, event | category | flops | bytes accessed | tf_op | source)
XLA Modules:
  0.0 62.4 jit_solution(13376043894758172281)
XLA Ops:
  0.6 59.0 %shard_map.220 = (bf16[8,768]{1,0:T(8,128)(2,1)S(1)}, bf16[8,768,192]{2,1,0:T(8,128)(2,1)S(1)}, bf16[8,768,192]{2,1,0:T(8,128)(2,1)S(1)}) custom-call(bf16[8,768]{1,0:T(8,128)(2,1)} %hid.1, bf16[8,768,192]{2,1,0:T(8,128)(2,1)} %bitcast.29, bf16[8,768,192]{2,1,0:T(8,128)(2,1)} %bitcast.30, bf16[8,768,384]{2,1,0:T(8,128)(2,1)} %bitcast.26, ...), custom_call_target="tpu_custom_call" | custom-call | tf_op jit(solution)/shard_map/pallas_call | solution.py:358
  59.7 2.7 %shard_map.221 = (bf16[8,768]{1,0:T(8,128)(2,1)}, bf16[8,768,192]{2,1,0:T(8,128)(2,1)}, bf16[8,768,192]{2,1,0:T(8,128)(2,1)}) custom-call(bf16[8,768]{1,0:T(8,128)(2,1)S(1)} %get-tuple-element.9.h_in, bf16[8,768,192]{2,1,0:T(8,128)(2,1)S(1)} %get-tuple-element.10.k_in, bf16[8,768,192]{2,1,0:T(8,128)(2,1)S(1)} %get-tuple-element.11.v_in), custom_call_target="tpu_custom_call" | custom-call | tf_op jit(solution)/shard_map/pallas_call | solution.py:369

commit v4 on v3

--- a/solution.py
+++ b/solution.py
@@ -23,6 +23,8 @@
 
 ALL_OFFS = [(kz, ky, kc) for kz in (2, 3, 1, 0) for ky in (1, 0) for kc in (1, 0) if (kz, ky, kc) != (0, 0, 0)]
 CHIP_OFFS = [off for off in ALL_OFFS if off[2] == 0]
+NEAR_FIRST = [(0, 1, 0), (1, 0, 0), (3, 0, 0), (1, 1, 0), (3, 1, 0), (2, 0, 0), (2, 1, 0)]
+SIBLING = (0, 0, 1)
 SUB_OFFS = [(0, 1, 1), (0, 1, 0), (0, 0, 1)]
 Z_OFFS = [(2, 0, 0), (3, 0, 0), (1, 0, 0)]
 
@@ -63,8 +65,9 @@
            out_h, k_v, v_v,
            ck_v, cv_v, win_v, wout_v, mask_v, rel_v, ln1_v, ln2_v, ln3_v, wqkv, m1, ix, st2, r2, wgo, wgq, wgc, rw,
            c3, r4, st5, r5, c6, r7, st8, r8, st9, r9, bias_s, s_self, s_cross, ctx_v, h2_v, x3_v, u_v,
-           ld, snd, rcv):
+           ld, snd, rcv, direct):
     me = lax.axis_index('ws')
+    dpi = lax.axis_index('dp')
     z = me // 4
     s = me % 4
     y = s // 2
@@ -82,7 +85,40 @@
         return pltpu.make_async_remote_copy(src_ref=buf, dst_ref=buf, send_sem=snd.at[ph], recv_sem=rcv.at[ph],
                                             device_id={'ws': me}, device_id_type=MESH)
 
+    def gather_start(buf, ph, row):
+        for off in CHIP_OFFS:
+            k = NEAR_FIRST.index(off)
+            pltpu.make_async_remote_copy(src_ref=buf.at[me], dst_ref=buf.at[me], send_sem=snd.at[ph],
+                                         recv_sem=direct.at[row, k], device_id={'ws': peer_of(off)},
+                                         device_id_type=MESH).start()
+        send(buf.at[me], buf.at[me], ph, SIBLING)
+
+    def gather_finish(buf, ph, row):
+        for k, (kz, ky, kc) in enumerate(NEAR_FIRST):
+            src = peer_of((4 - kz, ky, 0))
+            pltpu.make_async_remote_copy(src_ref=buf.at[src], dst_ref=buf.at[src], send_sem=snd.at[ph],
+                                         recv_sem=direct.at[row, k], device_id={'ws': me},
+                                         device_id_type=MESH).wait_recv()
+            send(buf.at[src], buf.at[src], ph, SIBLING)
+        desc(buf.at[pl.ds(0, 8)], ph).wait_recv()
+
+    def weight_start(w, ph):
+        for off in Z_OFFS:
+            send(w.at[z, dpi], w.at[z, dpi], ph, off)
+
+    def weight_pass(w, ph):
+        desc(w.at[pl.ds(0, 3), 0], ph).wait_recv()
+        for kz in (1, 2, 3):
+            src = (z + kz) % 4
+            pltpu.make_async_remote_copy(src_ref=w.at[src, dpi], dst_ref=w.at[src, dpi], send_sem=snd.at[ph + 11],
+                                         recv_sem=rcv.at[ph + 11], device_id={'dp': 1 - dpi, 'ws': me},
+                                         device_id_type=MESH).start()
+
+    def weight_finish(w, ph):
+        desc(w.at[pl.ds(0, 3), 0], ph + 11).wait_recv()
+
     bar = pltpu.get_barrier_semaphore()
+    pl.semaphore_signal(bar, inc=1, device_id={'dp': 1 - dpi, 'ws': me}, device_id_type=MESH)
     for off in ALL_OFFS:
         pl.semaphore_signal(bar, inc=1, device_id={'ws': peer_of(off)}, device_id_type=MESH)
 
@@ -103,9 +139,12 @@
     load('rel', rel, rel_v)
     load('mask', mask, mask_v)
     load('wr', wr, rw.at[me])
-    load('wo', wo, wgo.at[z])
-    load('wqc', wqc, wgq.at[z])
-    load('woc', woc, wgc.at[z])
+    load('wo0', wo.at[pl.ds(0, CB // 2)], wgo.at[z, 0])
+    load('wo1', wo.at[pl.ds(CB // 2, CB // 2)], wgo.at[z, 1])
+    load('wqc0', wqc.at[pl.ds(0, CB // 2)], wgq.at[z, 0])
+    load('wqc1', wqc.at[pl.ds(CB // 2, CB // 2)], wgq.at[z, 1])
+    load('woc0', woc.at[pl.ds(0, CB // 2)], wgc.at[z, 0])
+    load('woc1', woc.at[pl.ds(CB // 2, CB // 2)], wgc.at[z, 1])
 
     row8 = iota((ROWS, 128), 0)
     idx_own = jnp.zeros((ROWS, 128), jnp.int32)
@@ -115,13 +154,12 @@
     ix[me] = idx_own.astype(BF16)
     wqkv[3 * CB:256, :] = jnp.zeros((256 - 3 * CB, D), BF16)
     loads['hid'].wait()
-    pl.semaphore_wait(bar, NDEV - 1)
-
-    for off in ALL_OFFS:
-        send(m1.at[me], m1.at[me], 0, off)
-    loads['wo'].wait()
-    for off in Z_OFFS:
-        send(wgo.at[z], wgo.at[z], 8, off)
+    pl.semaphore_wait(bar, NDEV)
+
+    gather_start(m1, 0, 0)
+    loads['wo0'].wait()
+    loads['wo1'].wait()
+    weight_start(wgo, 8)
     load('k', kT, k_v)
     load('v', vT, v_v)
 
@@ -142,19 +180,18 @@
         bb = bb + jnp.dot(rel_mid, pick, preferred_element_type=F32)
         bb = bb + jnp.dot(rel_lo, pick, preferred_element_type=F32)
         bias_s[b, 0:HEADS, :] = jnp.where(lane12 <= pos_s[b], bb, NEG)
-    for name in ('wq', 'wk', 'wv', 'ln1', 'ln2', 'ln3', 'wr', 'wqc', 'woc'):
+    for name in ('wq', 'wk', 'wv', 'ln1', 'ln2', 'ln3', 'wr', 'wqc0', 'wqc1', 'woc0', 'woc1'):
         loads[name].wait()
 
-    desc(m1.at[pl.ds(0, NDEV - 1)], 0).wait_recv()
+    gather_finish(m1, 0, 0)
     hall = m1[...].astype(F32).reshape(NDEV * ROWS, D)
     xn = rms(hall, ln1_v[...].reshape(1, D))
     st2[...] = dot_nt(xn, wqkv[...]).reshape(NDEV, ROWS, 256).astype(BF16)
     r2[me] = st2[me]
     for off in ALL_OFFS:
         send(st2.at[peer_of(off)], r2.at[me], 1, off)
-    for i, w in enumerate((wgq, wgc)):
-        for off in Z_OFFS:
-            send(w.at[z], w.at[z], 9 + i, off)
+    weight_start(wgq, 9)
+    weight_start(wgc, 10)
     for off in ALL_OFFS:
         send(ix.at[me], ix.at[me], 12, off)
         send(rw.at[me], rw.at[me], 11, off)
@@ -172,6 +209,7 @@
     loads['k'].wait()
     loads['v'].wait()
     desc(r2.at[pl.ds(0, NDEV - 1)], 1).wait_recv()
+    weight_pass(wgo, 8)
     rv = r2[...].astype(F32)
 
     def columns(lo):
@@ -200,16 +238,17 @@
 
     c3[s] = ctx_v[...].astype(BF16)
     subgroup(c3, 2)
+    weight_pass(wgq, 9)
     load('win', win, win_v)
     load('wout', wout, wout_v)
-    desc(wgo.at[pl.ds(0, 3)], 8).wait_recv()
     desc(c3.at[pl.ds(0, 3)], 2).wait_recv()
+    weight_finish(wgo, 8)
     ctx = c3[...].astype(F32).reshape(4 * ROWS, D).astype(BF16)
     h1_blk = (h_blk + dot_nt(ctx, wgo[...].reshape(4 * CB, D))).astype(BF16)
     r4[s, :, 0:4 * CB] = h1_blk
     subgroup(r4, 3)
-    desc(wgq.at[pl.ds(0, 3)], 9).wait_recv()
     desc(r4.at[pl.ds(0, 3)], 3).wait_recv()
+    weight_finish(wgq, 9)
     r4f = r4[...].astype(F32)
     h1 = natural([r4f[t] for t in range(4)])
     x2 = rms(h1, ln2_v[...].reshape(1, D))
@@ -218,6 +257,7 @@
     for off in SUB_OFFS:
         kz, ky, kc = off
         send(st5.at[((y + ky) % 2) * 2 + (c + kc) % 2], r5.at[s], 4, off)
+    weight_pass(wgc, 10)
     loads['ck'].wait()
     loads['cv'].wait()
     desc(r5.at[pl.ds(0, 3)], 4).wait_recv()
@@ -227,15 +267,14 @@
 
     c6[s] = ctx_v[...].astype(BF16)
     subgroup(c6, 5)
-    desc(wgc.at[pl.ds(0, 3)], 10).wait_recv()
     desc(c6.at[pl.ds(0, 3)], 5).wait_recv()
+    weight_finish(wgc, 10)
     ctx2 = c6[...].astype(F32).reshape(4 * ROWS, D).astype(BF16)
     h2_blk = (h1_blk.astype(F32) + dot_nt(ctx2, wgc[...].reshape(4 * CB, D))).astype(BF16)
     h2_f = h2_blk.astype(F32)
     r7[me, 0:32, :] = h2_f[:, 0:128].astype(BF16)
     r7[me, 32:48, :] = jnp.concatenate([h2_f[0:16, 128:192], h2_f[16:32, 128:192]], axis=-1).astype(BF16)
-    for off in ALL_OFFS:
-        send(r7.at[me], r7.at[me], 6, off)
+    gather_start(r7, 6, 1)
     desc(ix.at[pl.ds(0, NDEV - 1)], 12).wait_recv()
     idx_all = ix[...].astype(F32).reshape(NDEV * ROWS, 128)
     idx_t = idx_all.T
@@ -243,7 +282,7 @@
     slot = jnp.sum(jnp.where(earlier, 1.0, 0.0), axis=-1, keepdims=True)
     loads['win'].wait()
     loads['wout'].wait()
-    desc(r7.at[pl.ds(0, NDEV - 1)], 6).wait_recv()
+    gather_finish(r7, 6, 1)
     for t in range(4):
         h2g = natural([unpack(r7[4 * t + u].astype(F32)) for u in range(4)])
         h2_v[32 * t:32 * t + 32, :] = h2g
@@ -255,14 +294,13 @@
         hh = dot_nt(x3, win_v[2 * p:2 * p + 2].reshape(384, D))
         u_v[:, 384 * p:384 * p + 384] = jnp.where(idx3 == half + float(2 * p), jnp.maximum(hh, 0.0), 0.0).astype(BF16)
     chip = me // 2
-    sibling = (0, 0, 1)
 
     def partial(n):
         yn = jnp.dot(u_v[...], wout_v[:, :, 256 * n:256 * n + 256].reshape(NDEV * 192, 256),
                      preferred_element_type=F32).reshape(8, 2, ROWS, 256)
         st8[n, 0] = yn[:, 0]
         st8[n, 1] = yn[:, 1]
-        send(st8.at[n, 1 - c], r8.at[n], 13 + n, sibling)
+        send(st8.at[n, 1 - c], r8.at[n], 13 + n, SIBLING)
 
     def reduce_send(n):
         desc(r8.at[n], 13 + n).wait_recv()
@@ -298,8 +336,11 @@
     for n in range(3):
         desc(st9.at[n, pl.ds(0, 7)], 16 + n).wait_send()
         desc(r8.at[n], 13 + n).wait_send()
-    for buf, ph in ((c3, 2), (r4, 3), (st5, 4), (c6, 5), (wgo, 8), (wgq, 9), (wgc, 10)):
+    for buf, ph in ((c3, 2), (r4, 3), (st5, 4), (c6, 5)):
         desc(buf.at[pl.ds(0, 3)], ph).wait_send()
+    for w, ph in ((wgo, 8), (wgq, 9), (wgc, 10)):
+        desc(w.at[pl.ds(0, 3), 0], ph).wait_send()
+        desc(w.at[pl.ds(0, 3), 0], ph + 11).wait_send()
 
 
 def store(h_in, k_in, v_in, h_out, k_out, v_out, sem):
@@ -347,13 +388,14 @@
             V((ROWS, D, LC), BF16), V((ROWS, D, LC), BF16), V((NDEV, 192, D), BF16), V((NDEV, 192, D), BF16),
             V((ROWS, LC), jnp.int32), V((HEADS, LS), F32), V((D,), F32), V((D,), F32), V((D,), F32), V((256, D), BF16),
             V((NDEV, ROWS, D), BF16), V((NDEV, ROWS, 128), BF16), V((NDEV, ROWS, 256), BF16), V((NDEV, ROWS, 256), BF16),
-            V((4, CB, D), BF16), V((4, CB, D), BF16), V((4, CB, D), BF16), V((NDEV, 1, D), F32),
+            V((4, 2, CB // 2, D), BF16), V((4, 2, CB // 2, D), BF16), V((4, 2, CB // 2, D), BF16), V((NDEV, 1, D), F32),
             V((4, ROWS, D), BF16), V((4, 4 * ROWS, 256), BF16), V((4, ROWS, 256), BF16), V((4, ROWS, 256), BF16),
             V((4, ROWS, D), BF16), V((NDEV, CB, 128), BF16), V((3, 2, 8, ROWS, 256), F32), V((3, 8, ROWS, 256), F32),
             V((3, 8, ROWS, 256), F32), V((3, 8, ROWS, 256), F32),
             V((ROWS, HPAD, LS), F32), V((ROWS, HPAD, LS), F32), V((ROWS, HPAD, LC), F32), V((ROWS, D), F32),
             V((NDEV * ROWS, D), F32), V((NDEV * ROWS, D), F32), V((NDEV * ROWS, NDEV * 192), BF16),
-            pltpu.SemaphoreType.DMA((19,)), pltpu.SemaphoreType.DMA((19,)), pltpu.SemaphoreType.DMA((19,)),
+            pltpu.SemaphoreType.DMA((22,)), pltpu.SemaphoreType.DMA((22,)), pltpu.SemaphoreType.DMA((22,)),
+            pltpu.SemaphoreType.DMA((2, 7)),
         ]
         h_out, k_out, v_out = pl.pallas_call(
             kernel,

time: 62.7 us -> 53.8 us (0.86)
  Pallas kernels: 61.8 us -> 53 us
    pallas_call x1, Pallas kernels: 59 us -> 50.2 us  [block(): pl.pallas_call(kernel, out_shape=(V((ROWS, D), BF16), V((ROWS, D, LS), BF...]
where the time goes in v4:
time: 53.8 us; the launch traced here: 53.6 us
  Pallas kernels  53 us (99%)
  between operations  0.65 us (1%)
    pallas_call x1, Pallas kernels, block(): pl.pallas_call(kernel, out_shape=(V((ROWS, D), BF16), V((ROWS, D, LS), BF...  50.2 us
    pallas_call x1, Pallas kernels, block(): pl.pallas_call(store, out_shape=outs, in_specs=[vmem] * 3, out_specs=(any...  2.73 us

profile of v4, /device:TPU:0, one launch (start us, length us, event | category | flops | bytes accessed | tf_op | source)
XLA Modules:
  0.0 53.6 jit_solution(4601128626698975800)
XLA Ops:
  0.6 50.2 %shard_map.220 = (bf16[8,768]{1,0:T(8,128)(2,1)S(1)}, bf16[8,768,192]{2,1,0:T(8,128)(2,1)S(1)}, bf16[8,768,192]{2,1,0:T(8,128)(2,1)S(1)}) custom-call(bf16[8,768]{1,0:T(8,128)(2,1)} %hid.1, bf16[8,768,192]{2,1,0:T(8,128)(2,1)} %bitcast.29, bf16[8,768,192]{2,1,0:T(8,128)(2,1)} %bitcast.30, bf16[8,768,384]{2,1,0:T(8,128)(2,1)} %bitcast.26, ...), custom_call_target="tpu_custom_call" | custom-call | tf_op jit(solution)/shard_map/pallas_call | solution.py:400
  50.9 2.7 %shard_map.221 = (bf16[8,768]{1,0:T(8,128)(2,1)}, bf16[8,768,192]{2,1,0:T(8,128)(2,1)}, bf16[8,768,192]{2,1,0:T(8,128)(2,1)}) custom-call(bf16[8,768]{1,0:T(8,128)(2,1)S(1)} %get-tuple-element.9.h_in, bf16[8,768,192]{2,1,0:T(8,128)(2,1)S(1)} %get-tuple-element.10.k_in, bf16[8,768,192]{2,1,0:T(8,128)(2,1)S(1)} %get-tuple-element.11.v_in), custom_call_target="tpu_custom_call" | custom-call | tf_op jit(solution)/shard_map/pallas_call | solution.py:411

commit v5 on v4

--- a/solution.py
+++ b/solution.py
@@ -48,24 +48,42 @@
     return (col >= row) & (col < row + 64)
 
 
-def attention(q8, k_ref, v_ref, bias_of, s_ref, ctx_ref):
+def attention(q8, k_ref, v_ref, bias_of, s_ref, ctx_ref, q_ref, patch=None):
     hm = head_mask()
     for b in range(ROWS):
         qb = jnp.where(hm, jnp.broadcast_to(q8[b:b + 1, :], (HPAD, D)), 0.0).astype(BF16)
-        s_ref[b] = jnp.dot(qb, k_ref[b], preferred_element_type=F32) + bias_of(b)
+        q_ref[b] = qb
+    if patch is not None:
+        k8, v8, hit_of = patch
+        new = dot_nt(q_ref[...].reshape(ROWS * HPAD, D), k8.astype(BF16))
+        row = iota((ROWS * HPAD, ROWS), 0)
+        col = iota((ROWS * HPAD, ROWS), 1) * HPAD
+        new = jnp.sum(jnp.where((row >= col) & (row < col + HPAD), new, 0.0), axis=-1, keepdims=True)
+    for b in range(ROWS):
+        sb = jnp.dot(q_ref[b], k_ref[b], preferred_element_type=F32)
+        if patch is not None:
+            sb = jnp.where(hit_of(b), new[b * HPAD:(b + 1) * HPAD], sb)
+        s_ref[b] = sb + bias_of(b)
     s = s_ref[...]
     p = jnp.exp(s - jnp.max(s, axis=-1, keepdims=True))
     s_ref[...] = p / jnp.sum(p, axis=-1, keepdims=True)
     for b in range(ROWS):
-        cb = dot_nt(s_ref[b].astype(BF16), v_ref[b])
+        pb = s_ref[b].astype(BF16)
+        if patch is None:
+            cb = dot_nt(pb, v_ref[b])
+        else:
+            pf = pb.astype(F32)
+            hit = hit_of(b)
+            at_pos = jnp.sum(jnp.where(hit, pf, 0.0), axis=-1, keepdims=True)
+            cb = dot_nt(jnp.where(hit, 0.0, pf).astype(BF16), v_ref[b]) + at_pos * v8[b:b + 1, :]
         ctx_ref[b:b + 1, :] = jnp.sum(jnp.where(hm, cb, 0.0), axis=0, keepdims=True)
 
 
-def kernel(hid, kT, vT, ckT, cvT, pos_s, mask, rel, idx_s, ln1, ln2, ln3, wq, wk, wv, wo, wqc, woc, wr, win, wout,
+def kernel(hid, kT, vT, ckT, cvT, pos, mask, rel, idx, ln1, ln2, ln3, wq, wk, wv, wo, wqc, woc, wr, win, wout,
            out_h, k_v, v_v,
            ck_v, cv_v, win_v, wout_v, mask_v, rel_v, ln1_v, ln2_v, ln3_v, wqkv, m1, ix, st2, r2, wgo, wgq, wgc, rw,
            c3, r4, st5, r5, c6, r7, st8, r8, st9, r9, bias_s, s_self, s_cross, ctx_v, h2_v, x3_v, u_v,
-           ld, snd, rcv, direct):
+           k_old, v_old, hs, q_v, pos_s, idx_s, ld, snd, rcv, direct, fwd):
     me = lax.axis_index('ws')
     dpi = lax.axis_index('dp')
     z = me // 4
@@ -91,7 +109,6 @@
             pltpu.make_async_remote_copy(src_ref=buf.at[me], dst_ref=buf.at[me], send_sem=snd.at[ph],
                                          recv_sem=direct.at[row, k], device_id={'ws': peer_of(off)},
                                          device_id_type=MESH).start()
-        send(buf.at[me], buf.at[me], ph, SIBLING)
 
     def gather_finish(buf, ph, row):
         for k, (kz, ky, kc) in enumerate(NEAR_FIRST):
@@ -102,6 +119,10 @@
             send(buf.at[src], buf.at[src], ph, SIBLING)
         desc(buf.at[pl.ds(0, 8)], ph).wait_recv()
 
+    def subgroup(buf, ph):
+        for off in SUB_OFFS:
+            send(buf.at[s], buf.at[s], ph, off)
+
     def weight_start(w, ph):
         for off in Z_OFFS:
             send(w.at[z, dpi], w.at[z, dpi], ph, off)
@@ -129,11 +150,13 @@
         cp.start()
         loads[name] = cp
 
-    load('hid', hid, m1.at[me])
+    load('hid', hid, hs.at[s])
+    load('ln1', ln1, ln1_v)
+    load('pos', pos, pos_s)
+    load('idx', idx, idx_s)
     load('wq', wq, wqkv.at[pl.ds(0, CB)])
     load('wk', wk, wqkv.at[pl.ds(CB, CB)])
     load('wv', wv, wqkv.at[pl.ds(2 * CB, CB)])
-    load('ln1', ln1, ln1_v)
     load('ln2', ln2, ln2_v)
     load('ln3', ln3, ln3_v)
     load('rel', rel, rel_v)
@@ -146,22 +169,28 @@
     load('woc0', woc.at[pl.ds(0, CB // 2)], wgc.at[z, 0])
     load('woc1', woc.at[pl.ds(CB // 2, CB // 2)], wgc.at[z, 1])
 
+    wqkv[3 * CB:256, :] = jnp.zeros((256 - 3 * CB, D), BF16)
+    loads['hid'].wait()
+    loads['ln1'].wait()
+    m1[me] = rms(hs[s].astype(F32), ln1_v[...].reshape(1, D))
+    pl.semaphore_wait(bar, NDEV)
+
+    gather_start(m1, 0, 0)
+    send(m1.at[me], m1.at[me], 0, SIBLING)
+    loads['wo0'].wait()
+    loads['wo1'].wait()
+    weight_start(wgo, 8)
+    subgroup(hs, 7)
+    load('k', kT, k_old)
+    load('v', vT, v_old)
+    loads['pos'].wait()
+    loads['idx'].wait()
     row8 = iota((ROWS, 128), 0)
     idx_own = jnp.zeros((ROWS, 128), jnp.int32)
     for i in range(ROWS):
         idx_own = jnp.where(row8 == i, idx_s[i], idx_own)
     idx_own = idx_own.astype(F32)
     ix[me] = idx_own.astype(BF16)
-    wqkv[3 * CB:256, :] = jnp.zeros((256 - 3 * CB, D), BF16)
-    loads['hid'].wait()
-    pl.semaphore_wait(bar, NDEV)
-
-    gather_start(m1, 0, 0)
-    loads['wo0'].wait()
-    loads['wo1'].wait()
-    weight_start(wgo, 8)
-    load('k', kT, k_v)
-    load('v', vT, v_v)
 
     loads['rel'].wait()
     loads['mask'].wait()
@@ -180,12 +209,11 @@
         bb = bb + jnp.dot(rel_mid, pick, preferred_element_type=F32)
         bb = bb + jnp.dot(rel_lo, pick, preferred_element_type=F32)
         bias_s[b, 0:HEADS, :] = jnp.where(lane12 <= pos_s[b], bb, NEG)
-    for name in ('wq', 'wk', 'wv', 'ln1', 'ln2', 'ln3', 'wr', 'wqc0', 'wqc1', 'woc0', 'woc1'):
+    for name in ('wq', 'wk', 'wv', 'ln2', 'ln3', 'wr', 'wqc0', 'wqc1', 'woc0', 'woc1'):
         loads[name].wait()
 
     gather_finish(m1, 0, 0)
-    hall = m1[...].astype(F32).reshape(NDEV * ROWS, D)
-    xn = rms(hall, ln1_v[...].reshape(1, D))
+    xn = m1[...].astype(F32).reshape(NDEV * ROWS, D).astype(BF16)
     st2[...] = dot_nt(xn, wqkv[...]).reshape(NDEV, ROWS, 256).astype(BF16)
     r2[me] = st2[me]
     for off in ALL_OFFS:
@@ -203,7 +231,8 @@
              + (sel_r >= 3 * CB).astype(jnp.int32))
     sel = (iota((4 * CB, D), 1) == sel_r + sel_q * (4 * CB - CB) + s * CB)
     sel = jnp.where(sel, 1.0, 0.0).astype(BF16)
-    h_sub = m1[pl.ds(4 * z, 4)].astype(F32).reshape(4 * ROWS, D).astype(BF16)
+    desc(hs.at[pl.ds(0, 3)], 7).wait_recv()
+    h_sub = hs[...].astype(F32).reshape(4 * ROWS, D).astype(BF16)
     h_blk = dot_nt(h_sub, sel)
 
     loads['k'].wait()
@@ -216,18 +245,18 @@
         return jnp.concatenate([rv[d, :, lo:lo + CB] for d in range(NDEV)], axis=-1)
 
     q8 = columns(0)
-    k_cols = columns(CB).T
-    v_cols = columns(2 * CB).T
-    lane_s = iota((D, LS), 1)
-    for b in range(ROWS):
-        hit = lane_s == pos_s[b]
-        k_v[b] = jnp.where(hit, jnp.broadcast_to(k_cols[:, b:b + 1], (D, LS)), k_v[b].astype(F32)).astype(BF16)
-        v_v[b] = jnp.where(hit, jnp.broadcast_to(v_cols[:, b:b + 1], (D, LS)), v_v[b].astype(F32)).astype(BF16)
-    attention(q8, k_v, v_v, lambda b: bias_s[b], s_self, ctx_v)
-
-    def subgroup(buf, ph):
-        for off in SUB_OFFS:
-            send(buf.at[s], buf.at[s], ph, off)
+    k8 = columns(CB)
+    v8 = columns(2 * CB)
+    lane_h = iota((HPAD, LS), 1)
+    attention(q8, k_old, v_old, lambda b: bias_s[b], s_self, ctx_v, q_v,
+              (k8, v8, lambda b: lane_h == pos_s[b]))
+
+    def update(new, old, out):
+        cols = new.T
+        lane_s = iota((D, LS), 1)
+        for b in range(ROWS):
+            out[b] = jnp.where(lane_s == pos_s[b], jnp.broadcast_to(cols[:, b:b + 1], (D, LS)),
+                               old[b].astype(F32)).astype(BF16)
 
     def natural(pieces):
         return jnp.concatenate([pieces[t][:, q * CB:(q + 1) * CB] for q in range(4) for t in range(4)], axis=-1)
@@ -238,7 +267,9 @@
 
     c3[s] = ctx_v[...].astype(BF16)
     subgroup(c3, 2)
+    update(k8, k_old, k_v)
     weight_pass(wgq, 9)
+    update(v8, v_old, v_v)
     load('win', win, win_v)
     load('wout', wout, wout_v)
     desc(c3.at[pl.ds(0, 3)], 2).wait_recv()
@@ -263,7 +294,7 @@
     desc(r5.at[pl.ds(0, 3)], 4).wait_recv()
     r5f = r5[...].astype(F32)
     q2 = natural([r5f[t] for t in range(4)])
-    attention(q2, ck_v, cv_v, lambda b: jnp.where(mask_v[b:b + 1, :] == 1, 0.0, NEG), s_cross, ctx_v)
+    attention(q2, ck_v, cv_v, lambda b: jnp.where(mask_v[b:b + 1, :] == 1, 0.0, NEG), s_cross, ctx_v, q_v)
 
     c6[s] = ctx_v[...].astype(BF16)
     subgroup(c6, 5)
@@ -274,7 +305,17 @@
     h2_f = h2_blk.astype(F32)
     r7[me, 0:32, :] = h2_f[:, 0:128].astype(BF16)
     r7[me, 32:48, :] = jnp.concatenate([h2_f[0:16, 128:192], h2_f[16:32, 128:192]], axis=-1).astype(BF16)
+
+    def one(buf, sem):
+        return pltpu.make_async_remote_copy(src_ref=buf, dst_ref=buf, send_sem=snd.at[6], recv_sem=sem,
+                                            device_id={'ws': me}, device_id_type=MESH)
+
+    def pass_on(src, k):
+        pltpu.make_async_remote_copy(src_ref=r7.at[src], dst_ref=r7.at[src], send_sem=snd.at[6], recv_sem=fwd.at[k],
+                                     device_id={'ws': peer_of(SIBLING)}, device_id_type=MESH).start()
+
     gather_start(r7, 6, 1)
+    pass_on(me, 7)
     desc(ix.at[pl.ds(0, NDEV - 1)], 12).wait_recv()
     idx_all = ix[...].astype(F32).reshape(NDEV * ROWS, 128)
     idx_t = idx_all.T
@@ -282,12 +323,31 @@
     slot = jnp.sum(jnp.where(earlier, 1.0, 0.0), axis=-1, keepdims=True)
     loads['win'].wait()
     loads['wout'].wait()
-    gather_finish(r7, 6, 1)
-    for t in range(4):
+
+    def arrive(k):
+        kz, ky, kc = NEAR_FIRST[k]
+        src = peer_of((4 - kz, ky, 0))
+        one(r7.at[src], direct.at[1, k]).wait_recv()
+        pass_on(src, k)
+
+    def group(kz, parts):
+        for k in parts:
+            one(r7.at[0], fwd.at[k]).wait_recv()
+        t = (z + 4 - kz) % 4
         h2g = natural([unpack(r7[4 * t + u].astype(F32)) for u in range(4)])
-        h2_v[32 * t:32 * t + 32, :] = h2g
-        x3_v[32 * t:32 * t + 32, :] = rms(h2g, ln3_v[...].reshape(1, D)).astype(F32)
-    x3 = x3_v[...].astype(BF16)
+        at = pl.ds(pl.multiple_of(32 * t, 32), 32)
+        h2_v[at, :] = h2g
+        x3_v[at, :] = rms(h2g, ln3_v[...].reshape(1, D))
+
+    for k in range(5):
+        arrive(k)
+    group(0, (7, 0))
+    arrive(5)
+    arrive(6)
+    group(1, (1, 3))
+    group(3, (2, 4))
+    group(2, (5, 6))
+    x3 = x3_v[...]
     idx3 = jnp.concatenate([idx_all, idx_all, idx_all], axis=-1)
     half = (iota((NDEV * ROWS, 384), 1) >= 192).astype(F32)
     for p in range(8):
@@ -311,14 +371,14 @@
 
     partial(0)
     partial(1)
+    partial(2)
     reduce_send(0)
-    partial(2)
     reduce_send(1)
     reduce_send(2)
 
     desc(rw.at[pl.ds(0, NDEV - 1)], 11).wait_recv()
-    x3_own = x3_v[pl.ds(pl.multiple_of(me * ROWS, ROWS), ROWS), :]
     h2_own = h2_v[pl.ds(pl.multiple_of(me * ROWS, ROWS), ROWS), :]
+    x3_own = rms(h2_own, ln3_v[...].reshape(1, D)).astype(F32)
     logits = dot_nt(x3_own, rw[...].reshape(NDEV, D), precision=lax.Precision.HIGHEST)
     ex = jnp.exp(logits - jnp.max(logits, axis=-1, keepdims=True))
     probs = ex / jnp.sum(ex, axis=-1, keepdims=True)
@@ -336,7 +396,7 @@
     for n in range(3):
         desc(st9.at[n, pl.ds(0, 7)], 16 + n).wait_send()
         desc(r8.at[n], 13 + n).wait_send()
-    for buf, ph in ((c3, 2), (r4, 3), (st5, 4), (c6, 5)):
+    for buf, ph in ((c3, 2), (r4, 3), (st5, 4), (c6, 5), (hs, 7)):
         desc(buf.at[pl.ds(0, 3)], ph).wait_send()
     for w, ph in ((wgo, 8), (wgq, 9), (wgc, 10)):
         desc(w.at[pl.ds(0, 3), 0], ph).wait_send()
@@ -364,7 +424,6 @@
     out_specs = (row_mat, cache, cache)
 
     any_spec = pl.BlockSpec(memory_space=pltpu.HBM)
-    smem = pl.BlockSpec(memory_space=pltpu.SMEM)
     vmem = pl.BlockSpec(memory_space=pltpu.VMEM)
 
     def block(hidden, self_k, self_v, cross_k, cross_v, positions, enc_mask, rel_bias, expert_idx,
@@ -381,8 +440,6 @@
                 wq_self.T, wk_self.T, wv_self.T, wo_self.T, wq_cross.T, wo_cross.T, w_router.T,
                 jnp.swapaxes(w_in, 1, 2), w_out)
         specs = [any_spec] * len(args)
-        specs[5] = smem
-        specs[8] = smem
         V = pltpu.VMEM
         scratch = [
             V((ROWS, D, LC), BF16), V((ROWS, D, LC), BF16), V((NDEV, 192, D), BF16), V((NDEV, 192, D), BF16),
@@ -393,9 +450,11 @@
             V((4, ROWS, D), BF16), V((NDEV, CB, 128), BF16), V((3, 2, 8, ROWS, 256), F32), V((3, 8, ROWS, 256), F32),
             V((3, 8, ROWS, 256), F32), V((3, 8, ROWS, 256), F32),
             V((ROWS, HPAD, LS), F32), V((ROWS, HPAD, LS), F32), V((ROWS, HPAD, LC), F32), V((ROWS, D), F32),
-            V((NDEV * ROWS, D), F32), V((NDEV * ROWS, D), F32), V((NDEV * ROWS, NDEV * 192), BF16),
-            pltpu.SemaphoreType.DMA((22,)), pltpu.SemaphoreType.DMA((22,)), pltpu.SemaphoreType.DMA((22,)),
-            pltpu.SemaphoreType.DMA((2, 7)),
+            V((NDEV * ROWS, D), F32), V((NDEV * ROWS, D), BF16), V((NDEV * ROWS, NDEV * 192), BF16),
+            V((ROWS, D, LS), BF16), V((ROWS, D, LS), BF16), V((4, ROWS, D), BF16), V((ROWS, HPAD, D), BF16),
+            pltpu.SMEM((ROWS,), jnp.int32), pltpu.SMEM((ROWS,), jnp.int32),
+            pltpu.SemaphoreType.DMA((24,)), pltpu.SemaphoreType.DMA((22,)), pltpu.SemaphoreType.DMA((22,)),
+            pltpu.SemaphoreType.DMA((2, 7)), pltpu.SemaphoreType.DMA((8,)),
         ]
         h_out, k_out, v_out = pl.pallas_call(
             kernel,

time: 53.8 us -> 53.8 us (level)
  no operation moved by 1% of the time
where the time goes in v5:
time: 53.8 us; the launch traced here: 53.6 us
  Pallas kernels  52.9 us (98%)
  between operations  0.65 us (1%)
    pallas_call x1, Pallas kernels, block(): pl.pallas_call(kernel, out_shape=(V((ROWS, D), BF16), V((ROWS, D, LS), BF...  50.2 us
    pallas_call x1, Pallas kernels, block(): pl.pallas_call(store, out_shape=outs, in_specs=[vmem] * 3, out_specs=(any...  2.73 us

profile of v5, /device:TPU:0, one launch (start us, length us, event | category | flops | bytes accessed | tf_op | source)
XLA Modules:
  0.0 53.6 jit_solution(6701376436575076946)
XLA Ops:
  0.6 50.2 %shard_map.220 = (bf16[8,768]{1,0:T(8,128)(2,1)S(1)}, bf16[8,768,192]{2,1,0:T(8,128)(2,1)S(1)}, bf16[8,768,192]{2,1,0:T(8,128)(2,1)S(1)}) custom-call(bf16[8,768]{1,0:T(8,128)(2,1)} %hid.1, bf16[8,768,192]{2,1,0:T(8,128)(2,1)} %bitcast.29, bf16[8,768,192]{2,1,0:T(8,128)(2,1)} %bitcast.30, bf16[8,768,384]{2,1,0:T(8,128)(2,1)} %bitcast.26, ...), custom_call_target="tpu_custom_call" | custom-call | tf_op jit(solution)/shard_map/pallas_call | solution.py:459
  50.8 2.7 %shard_map.221 = (bf16[8,768]{1,0:T(8,128)(2,1)}, bf16[8,768,192]{2,1,0:T(8,128)(2,1)}, bf16[8,768,192]{2,1,0:T(8,128)(2,1)}) custom-call(bf16[8,768]{1,0:T(8,128)(2,1)S(1)} %get-tuple-element.9.h_in, bf16[8,768,192]{2,1,0:T(8,128)(2,1)S(1)} %get-tuple-element.10.k_in, bf16[8,768,192]{2,1,0:T(8,128)(2,1)S(1)} %get-tuple-element.11.v_in), custom_call_target="tpu_custom_call" | custom-call | tf_op jit(solution)/shard_map/pallas_call | solution.py:470

commit v6 on v5

--- a/solution.py
+++ b/solution.py
@@ -23,7 +23,6 @@
 
 ALL_OFFS = [(kz, ky, kc) for kz in (2, 3, 1, 0) for ky in (1, 0) for kc in (1, 0) if (kz, ky, kc) != (0, 0, 0)]
 CHIP_OFFS = [off for off in ALL_OFFS if off[2] == 0]
-NEAR_FIRST = [(0, 1, 0), (1, 0, 0), (3, 0, 0), (1, 1, 0), (3, 1, 0), (2, 0, 0), (2, 1, 0)]
 SIBLING = (0, 0, 1)
 SUB_OFFS = [(0, 1, 1), (0, 1, 0), (0, 0, 1)]
 Z_OFFS = [(2, 0, 0), (3, 0, 0), (1, 0, 0)]
@@ -91,6 +90,14 @@
     y = s // 2
     c = s % 2
 
+    z_near = (z, z + 1 - 2 * (z % 2), 2 - z // 2, 3 * (1 - z // 2))
+    chip = me // 2
+
+    def chip_of(dist, ky):
+        return z_near[dist] * 2 + (y + ky) % 2
+
+    near_first = [(dist, ky) for dist in range(4) for ky in (0, 1)][1:]
+
     def peer_of(off):
         kz, ky, kc = off
         return ((z + kz) % 4) * 4 + ((y + ky) % 2) * 2 + (c + kc) % 2
@@ -104,20 +111,25 @@
                                             device_id={'ws': me}, device_id_type=MESH)
 
     def gather_start(buf, ph, row):
-        for off in CHIP_OFFS:
-            k = NEAR_FIRST.index(off)
+        for dist, ky in near_first[::-1]:
             pltpu.make_async_remote_copy(src_ref=buf.at[me], dst_ref=buf.at[me], send_sem=snd.at[ph],
-                                         recv_sem=direct.at[row, k], device_id={'ws': peer_of(off)},
-                                         device_id_type=MESH).start()
-
-    def gather_finish(buf, ph, row):
-        for k, (kz, ky, kc) in enumerate(NEAR_FIRST):
-            src = peer_of((4 - kz, ky, 0))
-            pltpu.make_async_remote_copy(src_ref=buf.at[src], dst_ref=buf.at[src], send_sem=snd.at[ph],
-                                         recv_sem=direct.at[row, k], device_id={'ws': me},
-                                         device_id_type=MESH).wait_recv()
-            send(buf.at[src], buf.at[src], ph, SIBLING)
-        desc(buf.at[pl.ds(0, 8)], ph).wait_recv()
+                                         recv_sem=direct.at[row, chip],
+                                         device_id={'ws': chip_of(dist, ky) * 2 + c}, device_id_type=MESH).start()
+        gather_pass(buf, ph, row, me, chip)
+
+    def gather_pass(buf, ph, row, src, src_chip):
+        pltpu.make_async_remote_copy(src_ref=buf.at[src], dst_ref=buf.at[src], send_sem=snd.at[ph],
+                                     recv_sem=fwd.at[row, src_chip],
+                                     device_id={'ws': peer_of(SIBLING)}, device_id_type=MESH).start()
+
+    def arrived(buf, ph, sem):
+        pltpu.make_async_remote_copy(src_ref=buf.at[0], dst_ref=buf.at[0], send_sem=snd.at[ph], recv_sem=sem,
+                                     device_id={'ws': me}, device_id_type=MESH).wait_recv()
+
+    def gather_step(buf, ph, row, dist, ky):
+        src_chip = chip_of(dist, ky)
+        arrived(buf, ph, direct.at[row, src_chip])
+        gather_pass(buf, ph, row, src_chip * 2 + c, src_chip)
 
     def subgroup(buf, ph):
         for off in SUB_OFFS:
@@ -176,10 +188,6 @@
     pl.semaphore_wait(bar, NDEV)
 
     gather_start(m1, 0, 0)
-    send(m1.at[me], m1.at[me], 0, SIBLING)
-    loads['wo0'].wait()
-    loads['wo1'].wait()
-    weight_start(wgo, 8)
     subgroup(hs, 7)
     load('k', kT, k_old)
     load('v', vT, v_old)
@@ -212,7 +220,15 @@
     for name in ('wq', 'wk', 'wv', 'ln2', 'ln3', 'wr', 'wqc0', 'wqc1', 'woc0', 'woc1'):
         loads[name].wait()
 
-    gather_finish(m1, 0, 0)
+    for dist, ky in near_first:
+        gather_step(m1, 0, 0, dist, ky)
+        if (dist, ky) == (1, 1):
+            loads['wo0'].wait()
+            loads['wo1'].wait()
+            weight_start(wgo, 8)
+    for dist in range(4):
+        for ky in (0, 1):
+            arrived(m1, 0, fwd.at[0, chip_of(dist, ky)])
     xn = m1[...].astype(F32).reshape(NDEV * ROWS, D).astype(BF16)
     st2[...] = dot_nt(xn, wqkv[...]).reshape(NDEV, ROWS, 256).astype(BF16)
     r2[me] = st2[me]
@@ -220,9 +236,6 @@
         send(st2.at[peer_of(off)], r2.at[me], 1, off)
     weight_start(wgq, 9)
     weight_start(wgc, 10)
-    for off in ALL_OFFS:
-        send(ix.at[me], ix.at[me], 12, off)
-        send(rw.at[me], rw.at[me], 11, off)
     load('ck', ckT, ck_v)
     load('cv', cvT, cv_v)
 
@@ -289,6 +302,9 @@
         kz, ky, kc = off
         send(st5.at[((y + ky) % 2) * 2 + (c + kc) % 2], r5.at[s], 4, off)
     weight_pass(wgc, 10)
+    for off in ALL_OFFS:
+        send(ix.at[me], ix.at[me], 12, off)
+        send(rw.at[me], rw.at[me], 11, off)
     loads['ck'].wait()
     loads['cv'].wait()
     desc(r5.at[pl.ds(0, 3)], 4).wait_recv()
@@ -306,16 +322,7 @@
     r7[me, 0:32, :] = h2_f[:, 0:128].astype(BF16)
     r7[me, 32:48, :] = jnp.concatenate([h2_f[0:16, 128:192], h2_f[16:32, 128:192]], axis=-1).astype(BF16)
 
-    def one(buf, sem):
-        return pltpu.make_async_remote_copy(src_ref=buf, dst_ref=buf, send_sem=snd.at[6], recv_sem=sem,
-                                            device_id={'ws': me}, device_id_type=MESH)
-
-    def pass_on(src, k):
-        pltpu.make_async_remote_copy(src_ref=r7.at[src], dst_ref=r7.at[src], send_sem=snd.at[6], recv_sem=fwd.at[k],
-                                     device_id={'ws': peer_of(SIBLING)}, device_id_type=MESH).start()
-
     gather_start(r7, 6, 1)
-    pass_on(me, 7)
     desc(ix.at[pl.ds(0, NDEV - 1)], 12).wait_recv()
     idx_all = ix[...].astype(F32).reshape(NDEV * ROWS, 128)
     idx_t = idx_all.T
@@ -324,37 +331,29 @@
     loads['win'].wait()
     loads['wout'].wait()
 
-    def arrive(k):
-        kz, ky, kc = NEAR_FIRST[k]
-        src = peer_of((4 - kz, ky, 0))
-        one(r7.at[src], direct.at[1, k]).wait_recv()
-        pass_on(src, k)
-
-    def group(kz, parts):
-        for k in parts:
-            one(r7.at[0], fwd.at[k]).wait_recv()
-        t = (z + 4 - kz) % 4
+    def group(dist):
+        for ky in (0, 1):
+            arrived(r7, 6, fwd.at[1, chip_of(dist, ky)])
+        t = z_near[dist]
         h2g = natural([unpack(r7[4 * t + u].astype(F32)) for u in range(4)])
         at = pl.ds(pl.multiple_of(32 * t, 32), 32)
         h2_v[at, :] = h2g
         x3_v[at, :] = rms(h2g, ln3_v[...].reshape(1, D))
 
-    for k in range(5):
-        arrive(k)
-    group(0, (7, 0))
-    arrive(5)
-    arrive(6)
-    group(1, (1, 3))
-    group(3, (2, 4))
-    group(2, (5, 6))
+    for dist, ky in near_first[:5]:
+        gather_step(r7, 6, 1, dist, ky)
+    group(0)
+    gather_step(r7, 6, 1, *near_first[5])
+    gather_step(r7, 6, 1, *near_first[6])
+    group(1)
+    group(2)
+    group(3)
     x3 = x3_v[...]
     idx3 = jnp.concatenate([idx_all, idx_all, idx_all], axis=-1)
     half = (iota((NDEV * ROWS, 384), 1) >= 192).astype(F32)
     for p in range(8):
         hh = dot_nt(x3, win_v[2 * p:2 * p + 2].reshape(384, D))
         u_v[:, 384 * p:384 * p + 384] = jnp.where(idx3 == half + float(2 * p), jnp.maximum(hh, 0.0), 0.0).astype(BF16)
-    chip = me // 2
-
     def partial(n):
         yn = jnp.dot(u_v[...], wout_v[:, :, 256 * n:256 * n + 256].reshape(NDEV * 192, 256),
                      preferred_element_type=F32).reshape(8, 2, ROWS, 256)
@@ -404,8 +403,10 @@
 
 
 def store(h_in, k_in, v_in, h_out, k_out, v_out, sem):
+    parts = [(src.at[:, :, lanes], dst.at[:, :, lanes]) for src, dst in ((k_in, k_out), (v_in, v_out))
+             for lanes in (pl.ds(0, 128), pl.ds(128, LS - 128))]
     copies = [pltpu.make_async_copy(src, dst, sem.at[i])
-              for i, (src, dst) in enumerate(((k_in, k_out), (v_in, v_out), (h_in, h_out)))]
+              for i, (src, dst) in enumerate(((h_in, h_out), *parts))]
     for cp in copies:
         cp.start()
     for cp in copies:
@@ -454,7 +455,7 @@
             V((ROWS, D, LS), BF16), V((ROWS, D, LS), BF16), V((4, ROWS, D), BF16), V((ROWS, HPAD, D), BF16),
             pltpu.SMEM((ROWS,), jnp.int32), pltpu.SMEM((ROWS,), jnp.int32),
             pltpu.SemaphoreType.DMA((24,)), pltpu.SemaphoreType.DMA((22,)), pltpu.SemaphoreType.DMA((22,)),
-            pltpu.SemaphoreType.DMA((2, 7)), pltpu.SemaphoreType.DMA((8,)),
+            pltpu.SemaphoreType.DMA((2, 8)), pltpu.SemaphoreType.DMA((2, 8)),
         ]
         h_out, k_out, v_out = pl.pallas_call(
             kernel,
@@ -469,7 +470,7 @@
                 jax.ShapeDtypeStruct((ROWS, D, LS), BF16))
         h_out, k_out, v_out = pl.pallas_call(
             store, out_shape=outs, in_specs=[vmem] * 3, out_specs=(any_spec,) * 3,
-            scratch_shapes=[pltpu.SemaphoreType.DMA((3,))],
+            scratch_shapes=[pltpu.SemaphoreType.DMA((5,))],
             compiler_params=pltpu.CompilerParams(vmem_limit_bytes=4 * 1024 * 1024),
         )(h_out, k_out, v_out)
         return h_out, unflat(k_out), unflat(v_out)

time: 53.8 us -> 56.4 us (1.048)
  Pallas kernels: 52.9 us -> 55.5 us
    pallas_call x1, Pallas kernels: 50.2 us -> 52.8 us  [block(): pl.pallas_call(kernel, out_shape=(V((ROWS, D), BF16), V((ROWS, D, LS), BF...]
where the time goes in v6:
time: 56.4 us; the launch traced here: 56.2 us
  Pallas kernels  55.5 us (98%)
  between operations  0.65 us (1%)
    pallas_call x1, Pallas kernels, block(): pl.pallas_call(kernel, out_shape=(V((ROWS, D), BF16), V((ROWS, D, LS), BF...  52.8 us
    pallas_call x1, Pallas kernels, block(): pl.pallas_call(store, out_shape=outs, in_specs=[vmem] * 3, out_specs=(any...  2.75 us

profile of v6, /device:TPU:0, one launch (start us, length us, event | category | flops | bytes accessed | tf_op | source)
XLA Modules:
  0.0 56.2 jit_solution(13506777636397550466)
XLA Ops:
  0.6 52.8 %shard_map.220 = (bf16[8,768]{1,0:T(8,128)(2,1)S(1)}, bf16[8,768,192]{2,1,0:T(8,128)(2,1)S(1)}, bf16[8,768,192]{2,1,0:T(8,128)(2,1)S(1)}) custom-call(bf16[8,768]{1,0:T(8,128)(2,1)} %hid.1, bf16[8,768,192]{2,1,0:T(8,128)(2,1)} %bitcast.29, bf16[8,768,192]{2,1,0:T(8,128)(2,1)} %bitcast.30, bf16[8,768,384]{2,1,0:T(8,128)(2,1)} %bitcast.26, ...), custom_call_target="tpu_custom_call" | custom-call | tf_op jit(solution)/shard_map/pallas_call | solution.py:460
  53.4 2.7 %shard_map.221 = (bf16[8,768]{1,0:T(8,128)(2,1)}, bf16[8,768,192]{2,1,0:T(8,128)(2,1)}, bf16[8,768,192]{2,1,0:T(8,128)(2,1)}) custom-call(bf16[8,768]{1,0:T(8,128)(2,1)S(1)} %get-tuple-element.9.h_in, bf16[8,768,192]{2,1,0:T(8,128)(2,1)S(1)} %get-tuple-element.10.k_in, bf16[8,768,192]{2,1,0:T(8,128)(2,1)S(1)} %get-tuple-element.11.v_in), custom_call_target="tpu_custom_call" | custom-call | tf_op jit(solution)/shard_map/pallas_call | solution.py:471

commit v7 on v6

--- a/solution.py
+++ b/solution.py
@@ -188,6 +188,9 @@
     pl.semaphore_wait(bar, NDEV)
 
     gather_start(m1, 0, 0)
+    loads['wo0'].wait()
+    loads['wo1'].wait()
+    weight_start(wgo, 8)
     subgroup(hs, 7)
     load('k', kT, k_old)
     load('v', vT, v_old)
@@ -222,10 +225,6 @@
 
     for dist, ky in near_first:
         gather_step(m1, 0, 0, dist, ky)
-        if (dist, ky) == (1, 1):
-            loads['wo0'].wait()
-            loads['wo1'].wait()
-            weight_start(wgo, 8)
     for dist in range(4):
         for ky in (0, 1):
             arrived(m1, 0, fwd.at[0, chip_of(dist, ky)])
@@ -282,6 +281,9 @@
     subgroup(c3, 2)
     update(k8, k_old, k_v)
     weight_pass(wgq, 9)
+    for off in ALL_OFFS:
+        send(ix.at[me], ix.at[me], 12, off)
+        send(rw.at[me], rw.at[me], 11, off)
     update(v8, v_old, v_v)
     load('win', win, win_v)
     load('wout', wout, wout_v)
@@ -302,9 +304,6 @@
         kz, ky, kc = off
         send(st5.at[((y + ky) % 2) * 2 + (c + kc) % 2], r5.at[s], 4, off)
     weight_pass(wgc, 10)
-    for off in ALL_OFFS:
-        send(ix.at[me], ix.at[me], 12, off)
-        send(rw.at[me], rw.at[me], 11, off)
     loads['ck'].wait()
     loads['cv'].wait()
     desc(r5.at[pl.ds(0, 3)], 4).wait_recv()
@@ -403,10 +402,8 @@
 
 
 def store(h_in, k_in, v_in, h_out, k_out, v_out, sem):
-    parts = [(src.at[:, :, lanes], dst.at[:, :, lanes]) for src, dst in ((k_in, k_out), (v_in, v_out))
-             for lanes in (pl.ds(0, 128), pl.ds(128, LS - 128))]
     copies = [pltpu.make_async_copy(src, dst, sem.at[i])
-              for i, (src, dst) in enumerate(((h_in, h_out), *parts))]
+              for i, (src, dst) in enumerate(((k_in, k_out), (v_in, v_out), (h_in, h_out)))]
     for cp in copies:
         cp.start()
     for cp in copies:
@@ -470,7 +467,7 @@
                 jax.ShapeDtypeStruct((ROWS, D, LS), BF16))
         h_out, k_out, v_out = pl.pallas_call(
             store, out_shape=outs, in_specs=[vmem] * 3, out_specs=(any_spec,) * 3,
-            scratch_shapes=[pltpu.SemaphoreType.DMA((5,))],
+            scratch_shapes=[pltpu.SemaphoreType.DMA((3,))],
             compiler_params=pltpu.CompilerParams(vmem_limit_bytes=4 * 1024 * 1024),
         )(h_out, k_out, v_out)
         return h_out, unflat(k_out), unflat(v_out)

time: 56.4 us -> 53.5 us (0.949)
  Pallas kernels: 55.5 us -> 52.6 us
    pallas_call x1, Pallas kernels: 52.8 us -> 49.9 us  [block(): pl.pallas_call(kernel, out_shape=(V((ROWS, D), BF16), V((ROWS, D, LS), BF...]
where the time goes in v7:
time: 53.5 us; the launch traced here: 53.3 us
  Pallas kernels  52.6 us (98%)
  between operations  0.65 us (1%)
    pallas_call x1, Pallas kernels, block(): pl.pallas_call(kernel, out_shape=(V((ROWS, D), BF16), V((ROWS, D, LS), BF...  49.9 us
    pallas_call x1, Pallas kernels, block(): pl.pallas_call(store, out_shape=outs, in_specs=[vmem] * 3, out_specs=(any...  2.73 us

profile of v7, /device:TPU:0, one launch (start us, length us, event | category | flops | bytes accessed | tf_op | source)
XLA Modules:
  0.0 53.3 jit_solution(18214159727812300370)
XLA Ops:
  0.6 49.9 %shard_map.220 = (bf16[8,768]{1,0:T(8,128)(2,1)S(1)}, bf16[8,768,192]{2,1,0:T(8,128)(2,1)S(1)}, bf16[8,768,192]{2,1,0:T(8,128)(2,1)S(1)}) custom-call(bf16[8,768]{1,0:T(8,128)(2,1)} %hid.1, bf16[8,768,192]{2,1,0:T(8,128)(2,1)} %bitcast.29, bf16[8,768,192]{2,1,0:T(8,128)(2,1)} %bitcast.30, bf16[8,768,384]{2,1,0:T(8,128)(2,1)} %bitcast.26, ...), custom_call_target="tpu_custom_call" | custom-call | tf_op jit(solution)/shard_map/pallas_call | solution.py:457
  50.5 2.7 %shard_map.221 = (bf16[8,768]{1,0:T(8,128)(2,1)}, bf16[8,768,192]{2,1,0:T(8,128)(2,1)}, bf16[8,768,192]{2,1,0:T(8,128)(2,1)}) custom-call(bf16[8,768]{1,0:T(8,128)(2,1)S(1)} %get-tuple-element.9.h_in, bf16[8,768,192]{2,1,0:T(8,128)(2,1)S(1)} %get-tuple-element.10.k_in, bf16[8,768,192]{2,1,0:T(8,128)(2,1)S(1)} %get-tuple-element.11.v_in), custom_call_target="tpu_custom_call" | custom-call | tf_op jit(solution)/shard_map/pallas_call | solution.py:468

commit v8 on v7

--- a/solution.py
+++ b/solution.py
@@ -329,53 +329,68 @@
     slot = jnp.sum(jnp.where(earlier, 1.0, 0.0), axis=-1, keepdims=True)
     loads['win'].wait()
     loads['wout'].wait()
+    half_lane = (iota((64, 384), 1) >= 192).astype(F32)
 
     def group(dist):
         for ky in (0, 1):
             arrived(r7, 6, fwd.at[1, chip_of(dist, ky)])
         t = z_near[dist]
         h2g = natural([unpack(r7[4 * t + u].astype(F32)) for u in range(4)])
-        at = pl.ds(pl.multiple_of(32 * t, 32), 32)
-        h2_v[at, :] = h2g
-        x3_v[at, :] = rms(h2g, ln3_v[...].reshape(1, D))
-
-    for dist, ky in near_first[:5]:
+        h2_v[32 * dist:32 * dist + 32, :] = h2g
+        x3_v[32 * dist:32 * dist + 32, :] = rms(h2g, ln3_v[...].reshape(1, D))
+
+    def hidden_units(hf):
+        rows = pl.ds(64 * hf, 64)
+        x3 = x3_v[rows, :]
+        idx_h = jnp.concatenate([ix[pl.ds(4 * z_near[2 * hf + i], 4)].astype(F32).reshape(32, 128) for i in (0, 1)],
+                                axis=0)
+        idx3 = jnp.concatenate([idx_h, idx_h, idx_h], axis=-1)
+        for p in range(8):
+            hh = dot_nt(x3, win_v[2 * p:2 * p + 2].reshape(384, D))
+            kept = idx3 == half_lane + float(2 * p)
+            u_v[rows, 384 * p:384 * p + 384] = jnp.where(kept, jnp.maximum(hh, 0.0), 0.0).astype(BF16)
+
+    def partial(hf, n):
+        yn = jnp.dot(u_v[pl.ds(64 * hf, 64), :], wout_v[:, :, 256 * n:256 * n + 256].reshape(NDEV * 192, 256),
+                     preferred_element_type=F32).reshape(4, 2, ROWS, 256)
+        st8[hf, n, 0] = yn[:, 0]
+        st8[hf, n, 1] = yn[:, 1]
+        send(st8.at[hf, n, 1 - c], r8.at[hf, n], 22 + 3 * hf + n, SIBLING)
+
+    def reduce_send(hf, n):
+        desc(r8.at[hf, n], 22 + 3 * hf + n).wait_recv()
+        st9[hf, n] = st8[hf, n, c] + r8[hf, n]
+        for dist in (2 * hf + 1, 2 * hf):
+            for ky in ((1,) if dist == 0 else (1, 0)):
+                part = 2 * (dist - 2 * hf) + (y + ky) % 2
+                ph = 28 + 3 * hf + n
+                pltpu.make_async_remote_copy(src_ref=st9.at[hf, n, part], dst_ref=r9.at[n, chip],
+                                             send_sem=snd.at[ph], recv_sem=rcv.at[ph],
+                                             device_id={'ws': chip_of(dist, ky) * 2 + c}, device_id_type=MESH).start()
+        if hf == 0:
+            r9[n, chip] = st9[0, n, y]
+
+    for dist, ky in near_first[:3]:
         gather_step(r7, 6, 1, dist, ky)
     group(0)
-    gather_step(r7, 6, 1, *near_first[5])
-    gather_step(r7, 6, 1, *near_first[6])
     group(1)
+    hidden_units(0)
+    for dist, ky in near_first[3:]:
+        gather_step(r7, 6, 1, dist, ky)
+    for n in range(3):
+        partial(0, n)
     group(2)
     group(3)
-    x3 = x3_v[...]
-    idx3 = jnp.concatenate([idx_all, idx_all, idx_all], axis=-1)
-    half = (iota((NDEV * ROWS, 384), 1) >= 192).astype(F32)
-    for p in range(8):
-        hh = dot_nt(x3, win_v[2 * p:2 * p + 2].reshape(384, D))
-        u_v[:, 384 * p:384 * p + 384] = jnp.where(idx3 == half + float(2 * p), jnp.maximum(hh, 0.0), 0.0).astype(BF16)
-    def partial(n):
-        yn = jnp.dot(u_v[...], wout_v[:, :, 256 * n:256 * n + 256].reshape(NDEV * 192, 256),
-                     preferred_element_type=F32).reshape(8, 2, ROWS, 256)
-        st8[n, 0] = yn[:, 0]
-        st8[n, 1] = yn[:, 1]
-        send(st8.at[n, 1 - c], r8.at[n], 13 + n, SIBLING)
-
-    def reduce_send(n):
-        desc(r8.at[n], 13 + n).wait_recv()
-        st9[n] = st8[n, c] + r8[n]
-        for off in CHIP_OFFS:
-            send(st9.at[n, peer_of(off) // 2], r9.at[n, chip], 16 + n, off)
-        r9[n, chip] = st9[n, chip]
-
-    partial(0)
-    partial(1)
-    partial(2)
-    reduce_send(0)
-    reduce_send(1)
-    reduce_send(2)
+    hidden_units(1)
+    for n in range(3):
+        partial(1, n)
+    for n in range(3):
+        reduce_send(0, n)
+    for n in range(3):
+        reduce_send(1, n)
 
     desc(rw.at[pl.ds(0, NDEV - 1)], 11).wait_recv()
-    h2_own = h2_v[pl.ds(pl.multiple_of(me * ROWS, ROWS), ROWS), :]
+    h2_own = h2_v[pl.ds(pl.multiple_of(s * ROWS, ROWS), ROWS), :]
     x3_own = rms(h2_own, ln3_v[...].reshape(1, D)).astype(F32)
     logits = dot_nt(x3_own, rw[...].reshape(NDEV, D), precision=lax.Precision.HIGHEST)
     ex = jnp.exp(logits - jnp.max(logits, axis=-1, keepdims=True))
@@ -385,15 +400,18 @@
     gate = jnp.where(slot < float(NDEV), gate, 0.0)
 
     for n in range(3):
-        desc(r9.at[n, pl.ds(0, 7)], 16 + n).wait_recv()
+        desc(r9.at[n, pl.ds(0, 3)], 28 + n).wait_recv()
+        desc(r9.at[n, pl.ds(0, 4)], 31 + n).wait_recv()
     yv = jnp.concatenate([jnp.sum(r9[n], axis=0) for n in range(3)], axis=-1).astype(BF16).astype(F32)
     out_h[...] = (h2_own + yv * gate).astype(BF16)
 
     for buf, ph in ((m1, 0), (st2, 1), (r7, 6), (rw, 11), (ix, 12)):
         desc(buf.at[pl.ds(0, NDEV - 1)], ph).wait_send()
     for n in range(3):
-        desc(st9.at[n, pl.ds(0, 7)], 16 + n).wait_send()
-        desc(r8.at[n], 13 + n).wait_send()
+        desc(r9.at[n, pl.ds(0, 3)], 28 + n).wait_send()
+        desc(r9.at[n, pl.ds(0, 4)], 31 + n).wait_send()
+        desc(r8.at[0, n], 22 + n).wait_send()
+        desc(r8.at[1, n], 25 + n).wait_send()
     for buf, ph in ((c3, 2), (r4, 3), (st5, 4), (c6, 5), (hs, 7)):
         desc(buf.at[pl.ds(0, 3)], ph).wait_send()
     for w, ph in ((wgo, 8), (wgq, 9), (wgc, 10)):
@@ -445,13 +463,13 @@
             V((NDEV, ROWS, D), BF16), V((NDEV, ROWS, 128), BF16), V((NDEV, ROWS, 256), BF16), V((NDEV, ROWS, 256), BF16),
             V((4, 2, CB // 2, D), BF16), V((4, 2, CB // 2, D), BF16), V((4, 2, CB // 2, D), BF16), V((NDEV, 1, D), F32),
             V((4, ROWS, D), BF16), V((4, 4 * ROWS, 256), BF16), V((4, ROWS, 256), BF16), V((4, ROWS, 256), BF16),
-            V((4, ROWS, D), BF16), V((NDEV, CB, 128), BF16), V((3, 2, 8, ROWS, 256), F32), V((3, 8, ROWS, 256), F32),
-            V((3, 8, ROWS, 256), F32), V((3, 8, ROWS, 256), F32),
+            V((4, ROWS, D), BF16), V((NDEV, CB, 128), BF16), V((2, 3, 2, 4, ROWS, 256), F32), V((2, 3, 4, ROWS, 256), F32),
+            V((2, 3, 4, ROWS, 256), F32), V((3, 8, ROWS, 256), F32),
             V((ROWS, HPAD, LS), F32), V((ROWS, HPAD, LS), F32), V((ROWS, HPAD, LC), F32), V((ROWS, D), F32),
             V((NDEV * ROWS, D), F32), V((NDEV * ROWS, D), BF16), V((NDEV * ROWS, NDEV * 192), BF16),
             V((ROWS, D, LS), BF16), V((ROWS, D, LS), BF16), V((4, ROWS, D), BF16), V((ROWS, HPAD, D), BF16),
             pltpu.SMEM((ROWS,), jnp.int32), pltpu.SMEM((ROWS,), jnp.int32),
-            pltpu.SemaphoreType.DMA((24,)), pltpu.SemaphoreType.DMA((22,)), pltpu.SemaphoreType.DMA((22,)),
+            pltpu.SemaphoreType.DMA((24,)), pltpu.SemaphoreType.DMA((34,)), pltpu.SemaphoreType.DMA((34,)),
             pltpu.SemaphoreType.DMA((2, 8)), pltpu.SemaphoreType.DMA((2, 8)),
         ]
         h_out, k_out, v_out = pl.pallas_call(

time: 53.5 us -> 56.2 us (1.050)
  Pallas kernels: 52.6 us -> 55.3 us
    pallas_call x1, Pallas kernels: 49.9 us -> 52.6 us  [block(): pl.pallas_call(kernel, out_shape=(V((ROWS, D), BF16), V((ROWS, D, LS), BF...]
where the time goes in v8:
time: 56.2 us; the launch traced here: 56 us
  Pallas kernels  55.3 us (98%)
  between operations  0.65 us (1%)
    pallas_call x1, Pallas kernels, block(): pl.pallas_call(kernel, out_shape=(V((ROWS, D), BF16), V((ROWS, D, LS), BF...  52.6 us
    pallas_call x1, Pallas kernels, block(): pl.pallas_call(store, out_shape=outs, in_specs=[vmem] * 3, out_specs=(any...  2.73 us

profile of v8, /device:TPU:0, one launch (start us, length us, event | category | flops | bytes accessed | tf_op | source)
XLA Modules:
  0.0 56.0 jit_solution(13075486814458014918)
XLA Ops:
  0.6 52.6 %shard_map.220 = (bf16[8,768]{1,0:T(8,128)(2,1)S(1)}, bf16[8,768,192]{2,1,0:T(8,128)(2,1)S(1)}, bf16[8,768,192]{2,1,0:T(8,128)(2,1)S(1)}) custom-call(bf16[8,768]{1,0:T(8,128)(2,1)} %hid.1, bf16[8,768,192]{2,1,0:T(8,128)(2,1)} %bitcast.29, bf16[8,768,192]{2,1,0:T(8,128)(2,1)} %bitcast.30, bf16[8,768,384]{2,1,0:T(8,128)(2,1)} %bitcast.26, ...), custom_call_target="tpu_custom_call" | custom-call | tf_op jit(solution)/shard_map/pallas_call | solution.py:475
  53.2 2.7 %shard_map.221 = (bf16[8,768]{1,0:T(8,128)(2,1)}, bf16[8,768,192]{2,1,0:T(8,128)(2,1)}, bf16[8,768,192]{2,1,0:T(8,128)(2,1)}) custom-call(bf16[8,768]{1,0:T(8,128)(2,1)S(1)} %get-tuple-element.9.h_in, bf16[8,768,192]{2,1,0:T(8,128)(2,1)S(1)} %get-tuple-element.10.k_in, bf16[8,768,192]{2,1,0:T(8,128)(2,1)S(1)} %get-tuple-element.11.v_in), custom_call_target="tpu_custom_call" | custom-call | tf_op jit(solution)/shard_map/pallas_call | solution.py:486

commit v9 on v7

--- a/solution.py
+++ b/solution.py
@@ -98,13 +98,19 @@
 
     near_first = [(dist, ky) for dist in range(4) for ky in (0, 1)][1:]
 
+    def far_first():
+        return [chip_of(dist, ky) * 2 + (c + kc) % 2 for dist in (3, 2, 1, 0) for ky in (1, 0) for kc in (1, 0)][:-1]
+
     def peer_of(off):
         kz, ky, kc = off
         return ((z + kz) % 4) * 4 + ((y + ky) % 2) * 2 + (c + kc) % 2
 
     def send(src, dst, ph, off):
+        send_to(src, dst, ph, peer_of(off))
+
+    def send_to(src, dst, ph, dev):
         pltpu.make_async_remote_copy(src_ref=src, dst_ref=dst, send_sem=snd.at[ph], recv_sem=rcv.at[ph],
-                                     device_id={'ws': peer_of(off)}, device_id_type=MESH).start()
+                                     device_id={'ws': dev}, device_id_type=MESH).start()
 
     def desc(buf, ph):
         return pltpu.make_async_remote_copy(src_ref=buf, dst_ref=buf, send_sem=snd.at[ph], recv_sem=rcv.at[ph],
@@ -231,10 +237,9 @@
     xn = m1[...].astype(F32).reshape(NDEV * ROWS, D).astype(BF16)
     st2[...] = dot_nt(xn, wqkv[...]).reshape(NDEV, ROWS, 256).astype(BF16)
     r2[me] = st2[me]
-    for off in ALL_OFFS:
-        send(st2.at[peer_of(off)], r2.at[me], 1, off)
+    for dev in far_first():
+        send_to(st2.at[dev], r2.at[me], 1, dev)
     weight_start(wgq, 9)
-    weight_start(wgc, 10)
     load('ck', ckT, ck_v)
     load('cv', cvT, cv_v)
 
@@ -251,6 +256,7 @@
     loads['v'].wait()
     desc(r2.at[pl.ds(0, NDEV - 1)], 1).wait_recv()
     weight_pass(wgo, 8)
+    weight_start(wgc, 10)
     rv = r2[...].astype(F32)
 
     def columns(lo):
@@ -272,6 +278,10 @@
 
     def natural(pieces):
         return jnp.concatenate([pieces[t][:, q * CB:(q + 1) * CB] for q in range(4) for t in range(4)], axis=-1)
+
+    def pack(buf, i, blk):
+        buf[i, 0:32, :] = blk[:, 0:128].astype(BF16)
+        buf[i, 32:48, :] = jnp.concatenate([blk[0:16, 128:192], blk[16:32, 128:192]], axis=-1).astype(BF16)
 
     def unpack(blk):
         tail = jnp.concatenate([blk[32:48, 0:64], blk[32:48, 64:128]], axis=0)
@@ -291,12 +301,12 @@
     weight_finish(wgo, 8)
     ctx = c3[...].astype(F32).reshape(4 * ROWS, D).astype(BF16)
     h1_blk = (h_blk + dot_nt(ctx, wgo[...].reshape(4 * CB, D))).astype(BF16)
-    r4[s, :, 0:4 * CB] = h1_blk
+    pack(r4, s, h1_blk.astype(F32))
     subgroup(r4, 3)
     desc(r4.at[pl.ds(0, 3)], 3).wait_recv()
     weight_finish(wgq, 9)
     r4f = r4[...].astype(F32)
-    h1 = natural([r4f[t] for t in range(4)])
+    h1 = natural([unpack(r4f[t]) for t in range(4)])
     x2 = rms(h1, ln2_v[...].reshape(1, D))
     st5[:, :, 0:4 * CB] = dot_nt(x2, wgq[...].reshape(4 * CB, D)).reshape(4, ROWS, 4 * CB).astype(BF16)
     r5[s] = st5[s]
@@ -317,9 +327,7 @@
     weight_finish(wgc, 10)
     ctx2 = c6[...].astype(F32).reshape(4 * ROWS, D).astype(BF16)
     h2_blk = (h1_blk.astype(F32) + dot_nt(ctx2, wgc[...].reshape(4 * CB, D))).astype(BF16)
-    h2_f = h2_blk.astype(F32)
-    r7[me, 0:32, :] = h2_f[:, 0:128].astype(BF16)
-    r7[me, 32:48, :] = jnp.concatenate([h2_f[0:16, 128:192], h2_f[16:32, 128:192]], axis=-1).astype(BF16)
+    pack(r7, me, h2_blk.astype(F32))
 
     gather_start(r7, 6, 1)
     desc(ix.at[pl.ds(0, NDEV - 1)], 12).wait_recv()
@@ -363,8 +371,9 @@
     def reduce_send(n):
         desc(r8.at[n], 13 + n).wait_recv()
         st9[n] = st8[n, c] + r8[n]
-        for off in CHIP_OFFS:
-            send(st9.at[n, peer_of(off) // 2], r9.at[n, chip], 16 + n, off)
+        for dist, ky in near_first[::-1]:
+            dest = chip_of(dist, ky)
+            send_to(st9.at[n, dest], r9.at[n, chip], 16 + n, dest * 2 + c)
         r9[n, chip] = st9[n, chip]
 
     partial(0)
@@ -444,7 +453,7 @@
             V((ROWS, LC), jnp.int32), V((HEADS, LS), F32), V((D,), F32), V((D,), F32), V((D,), F32), V((256, D), BF16),
             V((NDEV, ROWS, D), BF16), V((NDEV, ROWS, 128), BF16), V((NDEV, ROWS, 256), BF16), V((NDEV, ROWS, 256), BF16),
             V((4, 2, CB // 2, D), BF16), V((4, 2, CB // 2, D), BF16), V((4, 2, CB // 2, D), BF16), V((NDEV, 1, D), F32),
-            V((4, ROWS, D), BF16), V((4, 4 * ROWS, 256), BF16), V((4, ROWS, 256), BF16), V((4, ROWS, 256), BF16),
+            V((4, ROWS, D), BF16), V((4, CB, 128), BF16), V((4, ROWS, 256), BF16), V((4, ROWS, 256), BF16),
             V((4, ROWS, D), BF16), V((NDEV, CB, 128), BF16), V((3, 2, 8, ROWS, 256), F32), V((3, 8, ROWS, 256), F32),
             V((3, 8, ROWS, 256), F32), V((3, 8, ROWS, 256), F32),
             V((ROWS, HPAD, LS), F32), V((ROWS, HPAD, LS), F32), V((ROWS, HPAD, LC), F32), V((ROWS, D), F32),

time: 53.5 us -> 53.2 us (level)
  no operation moved by 1% of the time
where the time goes in v9:
time: 53.2 us; the launch traced here: 53 us
  Pallas kernels  52.4 us (98%)
  between operations  0.65 us (1%)
    pallas_call x1, Pallas kernels, block(): pl.pallas_call(kernel, out_shape=(V((ROWS, D), BF16), V((ROWS, D, LS), BF...  49.7 us
    pallas_call x1, Pallas kernels, block(): pl.pallas_call(store, out_shape=outs, in_specs=[vmem] * 3, out_specs=(any...  2.73 us

profile of v9, /device:TPU:0, one launch (start us, length us, event | category | flops | bytes accessed | tf_op | source)
XLA Modules:
  0.0 53.0 jit_solution(916487869727311802)
XLA Ops:
  0.6 49.7 %shard_map.220 = (bf16[8,768]{1,0:T(8,128)(2,1)S(1)}, bf16[8,768,192]{2,1,0:T(8,128)(2,1)S(1)}, bf16[8,768,192]{2,1,0:T(8,128)(2,1)S(1)}) custom-call(bf16[8,768]{1,0:T(8,128)(2,1)} %hid.1, bf16[8,768,192]{2,1,0:T(8,128)(2,1)} %bitcast.29, bf16[8,768,192]{2,1,0:T(8,128)(2,1)} %bitcast.30, bf16[8,768,384]{2,1,0:T(8,128)(2,1)} %bitcast.26, ...), custom_call_target="tpu_custom_call" | custom-call | tf_op jit(solution)/shard_map/pallas_call | solution.py:466
  50.3 2.7 %shard_map.221 = (bf16[8,768]{1,0:T(8,128)(2,1)}, bf16[8,768,192]{2,1,0:T(8,128)(2,1)}, bf16[8,768,192]{2,1,0:T(8,128)(2,1)}) custom-call(bf16[8,768]{1,0:T(8,128)(2,1)S(1)} %get-tuple-element.9.h_in, bf16[8,768,192]{2,1,0:T(8,128)(2,1)S(1)} %get-tuple-element.10.k_in, bf16[8,768,192]{2,1,0:T(8,128)(2,1)S(1)} %get-tuple-element.11.v_in), custom_call_target="tpu_custom_call" | custom-call | tf_op jit(solution)/shard_map/pallas_call | solution.py:477

commit v10 on v9

--- a/solution.py
+++ b/solution.py
@@ -252,10 +252,10 @@
     h_sub = hs[...].astype(F32).reshape(4 * ROWS, D).astype(BF16)
     h_blk = dot_nt(h_sub, sel)
 
+    weight_pass(wgo, 8)
     loads['k'].wait()
     loads['v'].wait()
     desc(r2.at[pl.ds(0, NDEV - 1)], 1).wait_recv()
-    weight_pass(wgo, 8)
     weight_start(wgc, 10)
     rv = r2[...].astype(F32)
 
@@ -289,8 +289,8 @@
 
     c3[s] = ctx_v[...].astype(BF16)
     subgroup(c3, 2)
+    weight_pass(wgq, 9)
     update(k8, k_old, k_v)
-    weight_pass(wgq, 9)
     for off in ALL_OFFS:
         send(ix.at[me], ix.at[me], 12, off)
         send(rw.at[me], rw.at[me], 11, off)

time: 53.2 us -> 53.2 us (level)
  no operation moved by 1% of the time
where the time goes in v10:
time: 53.2 us; the launch traced here: 53 us
  Pallas kernels  52.3 us (98%)
  between operations  0.65 us (1%)
    pallas_call x1, Pallas kernels, block(): pl.pallas_call(kernel, out_shape=(V((ROWS, D), BF16), V((ROWS, D, LS), BF...  49.6 us
    pallas_call x1, Pallas kernels, block(): pl.pallas_call(store, out_shape=outs, in_specs=[vmem] * 3, out_specs=(any...  2.73 us

profile of v10, /device:TPU:0, one launch (start us, length us, event | category | flops | bytes accessed | tf_op | source)
XLA Modules:
  0.0 53.0 jit_solution(12750394620849407816)
XLA Ops:
  0.6 49.6 %shard_map.220 = (bf16[8,768]{1,0:T(8,128)(2,1)S(1)}, bf16[8,768,192]{2,1,0:T(8,128)(2,1)S(1)}, bf16[8,768,192]{2,1,0:T(8,128)(2,1)S(1)}) custom-call(bf16[8,768]{1,0:T(8,128)(2,1)} %hid.1, bf16[8,768,192]{2,1,0:T(8,128)(2,1)} %bitcast.29, bf16[8,768,192]{2,1,0:T(8,128)(2,1)} %bitcast.30, bf16[8,768,384]{2,1,0:T(8,128)(2,1)} %bitcast.26, ...), custom_call_target="tpu_custom_call" | custom-call | tf_op jit(solution)/shard_map/pallas_call | solution.py:466
  50.2 2.7 %shard_map.221 = (bf16[8,768]{1,0:T(8,128)(2,1)}, bf16[8,768,192]{2,1,0:T(8,128)(2,1)}, bf16[8,768,192]{2,1,0:T(8,128)(2,1)}) custom-call(bf16[8,768]{1,0:T(8,128)(2,1)S(1)} %get-tuple-element.9.h_in, bf16[8,768,192]{2,1,0:T(8,128)(2,1)S(1)} %get-tuple-element.10.k_in, bf16[8,768,192]{2,1,0:T(8,128)(2,1)S(1)} %get-tuple-element.11.v_in), custom_call_target="tpu_custom_call" | custom-call | tf_op jit(solution)/shard_map/pallas_call | solution.py:477

commit v11 on v10

--- a/solution.py
+++ b/solution.py
@@ -196,7 +196,6 @@
     gather_start(m1, 0, 0)
     loads['wo0'].wait()
     loads['wo1'].wait()
-    weight_start(wgo, 8)
     subgroup(hs, 7)
     load('k', kT, k_old)
     load('v', vT, v_old)
@@ -231,6 +230,8 @@
 
     for dist, ky in near_first:
         gather_step(m1, 0, 0, dist, ky)
+        if (dist, ky) == (0, 1):
+            weight_start(wgo, 8)
     for dist in range(4):
         for ky in (0, 1):
             arrived(m1, 0, fwd.at[0, chip_of(dist, ky)])
@@ -411,8 +412,10 @@
 
 
 def store(h_in, k_in, v_in, h_out, k_out, v_out, sem):
+    parts = [(src.at[b], dst.at[b]) for b in range(ROWS) for src, dst in ((k_in, k_out), (v_in, v_out))]
+    parts.append((h_in, h_out))
     copies = [pltpu.make_async_copy(src, dst, sem.at[i])
-              for i, (src, dst) in enumerate(((k_in, k_out), (v_in, v_out), (h_in, h_out)))]
+              for i, (src, dst) in enumerate(parts)]
     for cp in copies:
         cp.start()
     for cp in copies:
@@ -476,7 +479,7 @@
                 jax.ShapeDtypeStruct((ROWS, D, LS), BF16))
         h_out, k_out, v_out = pl.pallas_call(
             store, out_shape=outs, in_specs=[vmem] * 3, out_specs=(any_spec,) * 3,
-            scratch_shapes=[pltpu.SemaphoreType.DMA((3,))],
+            scratch_shapes=[pltpu.SemaphoreType.DMA((2 * ROWS + 1,))],
             compiler_params=pltpu.CompilerParams(vmem_limit_bytes=4 * 1024 * 1024),
         )(h_out, k_out, v_out)
         return h_out, unflat(k_out), unflat(v_out)

time: 53.2 us -> 55.2 us (1.038)
  Pallas kernels: 52.3 us -> 54.3 us
    pallas_call x1, Pallas kernels: 49.6 us -> 51.5 us  [block(): pl.pallas_call(kernel, out_shape=(V((ROWS, D), BF16), V((ROWS, D, LS), BF...]
where the time goes in v11:
time: 55.2 us; the launch traced here: 54.9 us
  Pallas kernels  54.3 us (98%)
  between operations  0.65 us (1%)
    pallas_call x1, Pallas kernels, block(): pl.pallas_call(kernel, out_shape=(V((ROWS, D), BF16), V((ROWS, D, LS), BF...  51.5 us
    pallas_call x1, Pallas kernels, block(): pl.pallas_call(store, out_shape=outs, in_specs=[vmem] * 3, out_specs=(any...  2.79 us

profile of v11, /device:TPU:0, one launch (start us, length us, event | category | flops | bytes accessed | tf_op | source)
XLA Modules:
  0.0 54.9 jit_solution(13272633538208470310)
XLA Ops:
  0.6 51.5 %shard_map.220 = (bf16[8,768]{1,0:T(8,128)(2,1)S(1)}, bf16[8,768,192]{2,1,0:T(8,128)(2,1)S(1)}, bf16[8,768,192]{2,1,0:T(8,128)(2,1)S(1)}) custom-call(bf16[8,768]{1,0:T(8,128)(2,1)} %hid.1, bf16[8,768,192]{2,1,0:T(8,128)(2,1)} %bitcast.29, bf16[8,768,192]{2,1,0:T(8,128)(2,1)} %bitcast.30, bf16[8,768,384]{2,1,0:T(8,128)(2,1)} %bitcast.26, ...), custom_call_target="tpu_custom_call" | custom-call | tf_op jit(solution)/shard_map/pallas_call | solution.py:469
  52.1 2.8 %shard_map.221 = (bf16[8,768]{1,0:T(8,128)(2,1)}, bf16[8,768,192]{2,1,0:T(8,128)(2,1)}, bf16[8,768,192]{2,1,0:T(8,128)(2,1)}) custom-call(bf16[8,768]{1,0:T(8,128)(2,1)S(1)} %get-tuple-element.9.h_in, bf16[8,768,192]{2,1,0:T(8,128)(2,1)S(1)} %get-tuple-element.10.k_in, bf16[8,768,192]{2,1,0:T(8,128)(2,1)S(1)} %get-tuple-element.11.v_in), custom_call_target="tpu_custom_call" | custom-call | tf_op jit(solution)/shard_map/pallas_call | solution.py:480

commit v12 on v10

--- a/solution.py
+++ b/solution.py
@@ -141,9 +141,9 @@
         for off in SUB_OFFS:
             send(buf.at[s], buf.at[s], ph, off)
 
-    def weight_start(w, ph):
-        for off in Z_OFFS:
-            send(w.at[z, dpi], w.at[z, dpi], ph, off)
+    def weight_start(w, ph, dists=(3, 2, 1)):
+        for dist in dists:
+            send_to(w.at[z, dpi], w.at[z, dpi], ph, chip_of(dist, 0) * 2 + c)
 
     def weight_pass(w, ph):
         desc(w.at[pl.ds(0, 3), 0], ph).wait_recv()
@@ -196,7 +196,7 @@
     gather_start(m1, 0, 0)
     loads['wo0'].wait()
     loads['wo1'].wait()
-    weight_start(wgo, 8)
+    weight_start(wgo, 8, (3, 2))
     subgroup(hs, 7)
     load('k', kT, k_old)
     load('v', vT, v_old)
@@ -239,6 +239,7 @@
     r2[me] = st2[me]
     for dev in far_first():
         send_to(st2.at[dev], r2.at[me], 1, dev)
+    weight_start(wgo, 8, (1,))
     weight_start(wgq, 9)
     load('ck', ckT, ck_v)
     load('cv', cvT, cv_v)

time: 53.2 us -> 54.1 us (1.017)
  Pallas kernels: 52.3 us -> 53.3 us
    pallas_call x1, Pallas kernels: 49.6 us -> 50.5 us  [block(): pl.pallas_call(kernel, out_shape=(V((ROWS, D), BF16), V((ROWS, D, LS), BF...]
where the time goes in v12:
time: 54.1 us; the launch traced here: 53.9 us
  Pallas kernels  53.3 us (99%)
  between operations  0.65 us (1%)
    pallas_call x1, Pallas kernels, block(): pl.pallas_call(kernel, out_shape=(V((ROWS, D), BF16), V((ROWS, D, LS), BF...  50.5 us
    pallas_call x1, Pallas kernels, block(): pl.pallas_call(store, out_shape=outs, in_specs=[vmem] * 3, out_specs=(any...  2.73 us

profile of v12, /device:TPU:0, one launch (start us, length us, event | category | flops | bytes accessed | tf_op | source)
XLA Modules:
  0.0 53.9 jit_solution(17359017387646520297)
XLA Ops:
  0.6 50.5 %shard_map.220 = (bf16[8,768]{1,0:T(8,128)(2,1)S(1)}, bf16[8,768,192]{2,1,0:T(8,128)(2,1)S(1)}, bf16[8,768,192]{2,1,0:T(8,128)(2,1)S(1)}) custom-call(bf16[8,768]{1,0:T(8,128)(2,1)} %hid.1, bf16[8,768,192]{2,1,0:T(8,128)(2,1)} %bitcast.29, bf16[8,768,192]{2,1,0:T(8,128)(2,1)} %bitcast.30, bf16[8,768,384]{2,1,0:T(8,128)(2,1)} %bitcast.26, ...), custom_call_target="tpu_custom_call" | custom-call | tf_op jit(solution)/shard_map/pallas_call | solution.py:467
  51.2 2.7 %shard_map.221 = (bf16[8,768]{1,0:T(8,128)(2,1)}, bf16[8,768,192]{2,1,0:T(8,128)(2,1)}, bf16[8,768,192]{2,1,0:T(8,128)(2,1)}) custom-call(bf16[8,768]{1,0:T(8,128)(2,1)S(1)} %get-tuple-element.9.h_in, bf16[8,768,192]{2,1,0:T(8,128)(2,1)S(1)} %get-tuple-element.10.k_in, bf16[8,768,192]{2,1,0:T(8,128)(2,1)S(1)} %get-tuple-element.11.v_in), custom_call_target="tpu_custom_call" | custom-call | tf_op jit(solution)/shard_map/pallas_call | solution.py:478

commit v13 on v10

--- a/solution.py
+++ b/solution.py
@@ -142,8 +142,8 @@
             send(buf.at[s], buf.at[s], ph, off)
 
     def weight_start(w, ph):
-        for off in Z_OFFS:
-            send(w.at[z, dpi], w.at[z, dpi], ph, off)
+        for dist in (3, 2, 1):
+            send_to(w.at[z, dpi], w.at[z, dpi], ph, chip_of(dist, 0) * 2 + c)
 
     def weight_pass(w, ph):
         desc(w.at[pl.ds(0, 3), 0], ph).wait_recv()
@@ -291,10 +291,10 @@
     subgroup(c3, 2)
     weight_pass(wgq, 9)
     update(k8, k_old, k_v)
+    update(v8, v_old, v_v)
     for off in ALL_OFFS:
         send(ix.at[me], ix.at[me], 12, off)
         send(rw.at[me], rw.at[me], 11, off)
-    update(v8, v_old, v_v)
     load('win', win, win_v)
     load('wout', wout, wout_v)
     desc(c3.at[pl.ds(0, 3)], 2).wait_recv()

time: 53.2 us -> 53.3 us (level)
  no operation moved by 1% of the time
where the time goes in v13:
time: 53.3 us; the launch traced here: 53.1 us
  Pallas kernels  52.4 us (98%)
  between operations  0.65 us (1%)
    pallas_call x1, Pallas kernels, block(): pl.pallas_call(kernel, out_shape=(V((ROWS, D), BF16), V((ROWS, D, LS), BF...  49.7 us
    pallas_call x1, Pallas kernels, block(): pl.pallas_call(store, out_shape=outs, in_specs=[vmem] * 3, out_specs=(any...  2.73 us

profile of v13, /device:TPU:0, one launch (start us, length us, event | category | flops | bytes accessed | tf_op | source)
XLA Modules:
  0.0 53.1 jit_solution(118008520372425040)
XLA Ops:
  0.6 49.7 %shard_map.220 = (bf16[8,768]{1,0:T(8,128)(2,1)S(1)}, bf16[8,768,192]{2,1,0:T(8,128)(2,1)S(1)}, bf16[8,768,192]{2,1,0:T(8,128)(2,1)S(1)}) custom-call(bf16[8,768]{1,0:T(8,128)(2,1)} %hid.1, bf16[8,768,192]{2,1,0:T(8,128)(2,1)} %bitcast.29, bf16[8,768,192]{2,1,0:T(8,128)(2,1)} %bitcast.30, bf16[8,768,384]{2,1,0:T(8,128)(2,1)} %bitcast.26, ...), custom_call_target="tpu_custom_call" | custom-call | tf_op jit(solution)/shard_map/pallas_call | solution.py:466
  50.3 2.7 %shard_map.221 = (bf16[8,768]{1,0:T(8,128)(2,1)}, bf16[8,768,192]{2,1,0:T(8,128)(2,1)}, bf16[8,768,192]{2,1,0:T(8,128)(2,1)}) custom-call(bf16[8,768]{1,0:T(8,128)(2,1)S(1)} %get-tuple-element.9.h_in, bf16[8,768,192]{2,1,0:T(8,128)(2,1)S(1)} %get-tuple-element.10.k_in, bf16[8,768,192]{2,1,0:T(8,128)(2,1)S(1)} %get-tuple-element.11.v_in), custom_call_target="tpu_custom_call" | custom-call | tf_op jit(solution)/shard_map/pallas_call | solution.py:477
